TPU v7x, 32 devices: a whole 2x2x4 slice. The times are simulated.
32 devices in a mesh: beam: 4 (over y, x), row: 4 (over z), col: 2 (over core).
Axes of the slice: x: 2, y: 2, z: 4, core: 2. Of those that a mesh axis runs over, the one named last changes fastest.
Arguments:
- phase_volume: bfloat16 [64, 1024, 256], P('beam', 'row', 'col'), may hold values from -0.75 to 0.75
- absorb_volume: bfloat16 [64, 1024, 256], P('beam', 'row', 'col'), may hold values from -0.375 to 0.375
- probe: float32 [2, 256, 256], replicated, may hold values from -6 to 6
- amplitudes: bfloat16 [4, 2, 32, 256, 256], P('row', 'col', 'beam'), may hold values from 0.19921875 to 2.5
- scan_rows: int32 [4, 2, 32], P('row', 'col', 'beam'), may hold values from 0 to 255
- scan_cols: int32 [4, 2, 32], P('row', 'col', 'beam'), may hold values from 0 to 127
Outputs:
- object_step: float32 [2, 1024, 256], P(None, 'row', 'col')
- probe_gradient: float32 [2, 256, 256], replicated
- loss: float32 [], replicated
All inputs are finite; a program needn't handle non-finite values.
Results may differ from a plain program's by a relative error of at most 0.00055.
The roundings to bfloat16 on the way count: a program that leaves them out, or rounds other values in their place, can miss the bound.
Values sent between devices are 32-bit elements; how exact they have to be, the bound alone decides.
A program may use at most 64 MiB of HBM per device.

v0:
```python
import math

import jax
import jax.numpy as jnp
from jax import lax
from jax.sharding import PartitionSpec as P


def from_behind(value, axis, steps):
    count = lax.axis_size(axis)
    first, last = (max(0, -steps), min(count, count - steps))
    return lax.ppermute(value, axis, [(source, source + steps) for source in range(first, last)])


def extended(cells, sides, width):
    for axis, dim in sides:
        count = lax.axis_size(axis)
        ends = count - 1
        head = lax.slice_in_dim(cells, 0, width, axis=dim)
        tail = lax.slice_in_dim(cells, cells.shape[dim] - width, cells.shape[dim], axis=dim)
        cells = jnp.concatenate(
            [
                lax.ppermute(tail, axis, [(i, (i + 1) % count) for i in range(ends)]),
                cells,
                lax.ppermute(head, axis, [((i + 1) % count, i) for i in range(ends)]),
            ],
            axis=dim,
        )
    return cells


def dft_tables(length):
    indices = jnp.arange(length, dtype=jnp.int32)
    product = indices[:, None] * indices[None, :] % length
    angles = product.astype(jnp.float32) * (2.0 * math.pi / length)
    factor = 1.0 / math.sqrt(length)
    return (
        (jnp.cos(angles) * factor).astype(jnp.bfloat16),
        (-jnp.sin(angles) * factor).astype(jnp.bfloat16),
    )


def fold_rims(canvas, half):
    rows_inner = canvas.shape[1] - 2 * half
    cols_inner = canvas.shape[2] - 2 * half
    middle = canvas[:, :, half : half + cols_inner]
    from_right = from_behind(canvas[:, :, :half], "col", -1)
    from_left = from_behind(canvas[:, :, half + cols_inner :], "col", 1)
    middle = middle + from_right
    middle = middle + from_left
    center = middle[:, half : half + rows_inner, :]
    from_below = from_behind(middle[:, :half, :], "row", -1)
    from_above = from_behind(middle[:, half + rows_inner :, :], "row", 1)
    center = center + jnp.pad(from_below, ((0, 0), (rows_inner - half, 0), (0, 0)))
    return center + jnp.pad(from_above, ((0, 0), (0, rows_inner - half), (0, 0)))


def local(phase_volume, absorb_volume, probe, amplitudes, scan_rows, scan_cols):
    length = probe.shape[1]
    half = length // 2
    count = scan_rows.shape[2]
    rows_local = phase_volume.shape[1]
    cols_local = phase_volume.shape[2]
    phase_part = jnp.sum(phase_volume, axis=0, dtype=jnp.float32)
    absorb_part = jnp.sum(absorb_volume, axis=0, dtype=jnp.float32)
    phase_sum, absorb_sum = lax.psum((phase_part, absorb_part), "beam")
    padded = extended(jnp.stack([phase_sum, absorb_sum]), (("row", 1), ("col", 2)), half)
    row_begin = scan_rows.reshape(count)
    col_begin = scan_cols.reshape(count)
    zero_index = jnp.zeros((), jnp.int32)
    windows = jax.vmap(
        lambda row_at, col_at: lax.dynamic_slice(
            padded, (zero_index, row_at, col_at), (2, length, length)
        )
    )(row_begin, col_begin)
    table_real, table_imag = dft_tables(length)
    negated = -table_imag
    forward_left = jnp.stack(
        [jnp.stack([table_real, negated]), jnp.stack([table_imag, table_real])]
    )
    forward_right = jnp.stack(
        [
            jnp.concatenate([table_real, table_imag], axis=1),
            jnp.concatenate([negated, table_real], axis=1),
        ]
    )
    backward_left = jnp.stack(
        [jnp.stack([table_real, table_imag]), jnp.stack([negated, table_real])]
    )
    backward_right = jnp.stack(
        [
            jnp.concatenate([table_real, negated], axis=1),
            jnp.concatenate([table_imag, table_real], axis=1),
        ]
    )
    damping = jnp.exp(-windows[:, 1])
    trans_real = damping * jnp.cos(windows[:, 0])
    trans_imag = damping * jnp.sin(windows[:, 0])
    wave_real = probe[0] * trans_real - probe[1] * trans_imag
    wave_imag = probe[0] * trans_imag + probe[1] * trans_real
    outgoing = jnp.stack([wave_real, wave_imag], axis=1).astype(jnp.bfloat16)
    half_wave = jnp.einsum(
        "yxab,sxbc->syac", forward_left, outgoing, preferred_element_type=jnp.float32
    ).astype(jnp.bfloat16)
    far_field = jnp.einsum(
        "sxab,xbd->sad", half_wave, forward_right, preferred_element_type=jnp.float32
    )
    far_real = far_field[:, :, :length]
    far_imag = far_field[:, :, length:]
    amplitude = amplitudes.reshape(count, length, length).astype(jnp.float32)
    modulus = jnp.sqrt(far_real * far_real + far_imag * far_imag)
    misfit = jnp.sum((modulus - amplitude) * (modulus - amplitude))
    ratio = 1.0 - amplitude / jnp.maximum(modulus, 0.5)
    residual = (far_field * jnp.concatenate([ratio, ratio], axis=2)).astype(jnp.bfloat16)
    back_half = jnp.einsum(
        "yxab,sbxc->syac",
        backward_left,
        residual.reshape(count, length, 2, length),
        preferred_element_type=jnp.float32,
    ).astype(jnp.bfloat16)
    near_field = jnp.einsum(
        "syab,ybd->sad", back_half, backward_right, preferred_element_type=jnp.float32
    )
    grad_real = near_field[:, :, :length]
    grad_imag = near_field[:, :, length:]
    object_real = wave_real * grad_real + wave_imag * grad_imag
    object_imag = wave_real * grad_imag - wave_imag * grad_real
    cells = jnp.stack([object_imag, -object_real], axis=1)
    probe_term = jnp.stack(
        [
            jnp.sum(trans_real * grad_real + trans_imag * grad_imag, axis=0),
            jnp.sum(trans_real * grad_imag - trans_imag * grad_real, axis=0),
        ]
    )

    def add_window(index, canvas_now):
        where = (zero_index, row_begin[index], col_begin[index])
        piece = lax.dynamic_slice(canvas_now, where, (2, length, length))
        return lax.dynamic_update_slice(canvas_now, piece + cells[index], where)

    canvas = jnp.zeros((2, rows_local + length, cols_local + length), jnp.float32)
    canvas = lax.fori_loop(0, count, add_window, canvas)
    summed, probe_part, misfit_part = lax.psum((canvas, probe_term, misfit), "beam")
    probe_total, misfit_total = lax.psum((probe_part, misfit_part), ("row", "col"))
    gradient = fold_rims(summed, half)
    square_sum = lax.psum(jnp.sum(gradient * gradient), ("row", "col"))
    plane_devices = lax.axis_size("row") * lax.axis_size("col")
    mean_square = square_sum / (2 * rows_local * cols_local * plane_devices)
    factor = jnp.minimum(1.0, 0.5 / jnp.sqrt(mean_square + 1e-06))
    total = plane_devices * lax.axis_size("beam") * count
    return (gradient * factor, probe_total / total, misfit_total / (total * length * length))


def solution(mesh):
    in_specs = (
        P("beam", "row", "col"),
        P("beam", "row", "col"),
        P(),
        P("row", "col", "beam", None, None),
        P("row", "col", "beam"),
        P("row", "col", "beam"),
    )
    out_specs = (P(None, "row", "col"), P(), P())
    return jax.shard_map(local, mesh=mesh, in_specs=in_specs, out_specs=out_specs, check_vma=False)
```

profile of v0, /device:TPU:0, one launch (start us, length us, event | category | flops | bytes accessed | tf_op | source)
XLA Modules:
  0.0 417.0 jit_solution(9984468014252012961)
XLA Ops:
  13.5 43.8 %all-reduce.13.cloned.1.call-done = (f32[1,256,128]{2,1,0:T(8,128)}, f32[1,256,128]{2,1,0:T(8,128)}) async-done(((f32[1,256,128]{2,1,0:T(8,128)}, f32[1,256,128]{2,1,0:T(8,128)}), (f32[1,256,128]{2,1,0:T(8,128)}, f32[1,256,128]{2,1,0:T(8,128)})) %all-reduce.13.cloned.1.call-update) | async-done | bytes 262160 | tf_op jit(solution)/shard_map/psum | solution.py:66
  59.2 3.4 collective-permute-start
  66.0 3.4 collective-permute-done.1
  75.9 22.0 %while.15 = (s32[]{:T(128)}, f32[2,512,384]{2,1,0:T(8,128)S(1)}, s32[8,3]{0,1:T(4,128)S(1)}, f32[8,2,256,256]{3,2,0,1:T(8,128)}, s32[]{:T(128)}) while((s32[]{:T(128)}, f32[2,512,384]{2,1,0:T(8,128)S(1)}, s32[8,3]{0,1:T(4,128)S(1)}, f32[8,2,256,256]{3,2,0,1:T(8,128)}, s32[]{:T(128)}) %tuple.69), condition=%wide.while_cond, body=%wide.while_body.sunk | while | flops 2 | bytes 1050217 | solution.py:72
  97.9 9.9 %subtract_convert_fusion = (bf16[8,1,256,256]{3,2,0,1:T(8,128)(2,1)}, f32[8,1,256,256]{3,2,0,1:T(8,128)S(1)}, f32[8,1,256,256]{3,2,0,1:T(8,128)S(1)}) fusion(f32[256,256]{1,0:T(8,128)S(1)} %get-tuple-element.153, f32[256,256]{1,0:T(8,128)S(1)} %get-tuple-element.152, f32[8,2,256,256]{3,2,0,1:T(8,128)} %get-tuple-element.105), kind=kLoop, calls=%fused_computation.40 | loop fusion | flops 3670016 | bytes 9961472 | tf_op jit(solution)/shard_map/convert.1
  109.5 6.0 %convolution_bitcast_fusion.1 = f32[8,256,512]{2,1,0:T(8,128)} fusion(bf16[1,2,256,256]{3,2,1,0:T(8,128)(2,1)} %get-tuple-element.159, bf16[1,2,256,256]{3,2,1,0:T(8,128)(2,1)} %get-tuple-element.166, bf16[1,256,512]{2,1,0:T(8,128)(2,1)S(1)} %copy-done.6, bf16[1,256,512]{2,1,0:T(8,128)(2,1)S(1)} %copy-done.7, bf16[8,1,256,256]{3,2,0,1:T(8,128)(2,1)} %add_convert_fusion, ...), kind=kOutput, calls=%fused_computation.11 | convolution fusion | flops 2150891520 | bytes 7340032 | tf_op jit(solution)/shard_map/sxab,xbd->sad/dot_general | solution.py:105
  115.5 4.5 %fusion.3 = (f32[]{:T(128)}, f32[8,256,256]{2,1,0:T(8,128)S(1)}) fusion(bf16[1,1,8,256,256]{4,3,2,1,0:T(8,128)(2,1)} %param.11, f32[8,256,512]{2,1,0:T(8,128)} %convolution_bitcast_fusion.1), kind=kLoop, calls=%fused_computation.14 | loop fusion | flops 5242879 | bytes 7340036 | tf_op jit(solution)/shard_map/reduce_sum | solution.py:112
  121.9 4.0 copy.18
  125.9 5.9 %convolution_bitcast_fusion = f32[8,256,512]{2,1,0:T(8,128)} fusion(bf16[8,256,2,256,1]{1,3,2,4,0:T(8,128)(2,1)} %bitcast.155, bf16[1,2,256,256]{3,2,1,0:T(8,128)(2,1)} %get-tuple-element.167, bf16[1,2,256,256]{3,2,1,0:T(8,128)(2,1)S(1)} %copy-done.5, bf16[1,256,512]{2,1,0:T(8,128)(2,1)S(1)} %copy-done.4, bf16[1,256,512]{2,1,0:T(8,128)(2,1)S(1)} %get-tuple-element.154), kind=kOutput, calls=%fused_computation.10 | convolution fusion | flops 2149842944 | bytes 7340032 | tf_op jit(solution)/shard_map/syab,ybd->sad/dot_general | solution.py:121
  131.8 4.4 %fusion.11 = (f32[256,256]{1,0:T(8,128)S(1)}, f32[256,256]{1,0:T(8,128)S(1)}, f32[8,1,256,256]{3,2,0,1:T(8,128)S(1)}, f32[8,1,256,256]{3,2,0,1:T(8,128)S(1)}) fusion(f32[8,1,256,256]{3,2,0,1:T(8,128)S(1)} %get-tuple-element.138, f32[8,1,256,256]{3,2,0,1:T(8,128)} %copy-done.1, f32[8,256,512]{2,1,0:T(8,128)} %convolution_bitcast_fusion, ...), kind=kLoop, calls=%fused_computation.29 | loop fusion | flops 10878976 | bytes 13631488 | tf_op jit(solution)/shard_map/reduce_sum | solution.py:131
  138.5 115.7 %while.14 = (s32[]{:T(128)}, f32[2,512,384]{2,1,0:T(8,128)S(1)}, s32[8]{0:T(128)S(1)}, s32[8]{0:T(128)S(1)}, f32[8,2,256,256]{3,2,0,1:T(8,128)}, /*index=5*/s32[]{:T(128)}, s32[]{:T(128)}, s32[]{:T(128)}, s32[]{:T(128)}) while((s32[]{:T(128)}, f32[2,512,384]{2,1,0:T(8,128)S(1)}, s32[8]{0:T(128)S(1)}, s32[8]{0:T(128)S(1)}, ...), condition=%wide.region_5.6_spmd, body=%wide.region_4.5_spmd.sunk | while | flops 131080 | bytes 2621641 | solution.py:142
  144.8 7.3 %dynamic_update_slice.8 = f32[2,512,384]{2,1,0:T(8,128)S(1)} dynamic-update-slice(f32[2,512,384]{2,1,0:T(8,128)S(1)} %get-tuple-element.259, f32[2,256,256]{2,1,0:T(8,128)S(1)} %bitcast_add_fusion.2, s32[]{:T(128)} %constant.69.clone.1..sunk, s32[]{:T(128)S(6)} %select_n.125, s32[]{:T(128)S(6)} %select_n.126) | dynamic-update-slice | bytes 1048580 | tf_op jit(solution)/shard_map/while/body/eval_jaxpr/dynamic_update_slice | solution.py:139
  158.5 8.4 %dynamic_update_slice.8 = f32[2,512,384]{2,1,0:T(8,128)S(1)} dynamic-update-slice(f32[2,512,384]{2,1,0:T(8,128)S(1)} %get-tuple-element.259, f32[2,256,256]{2,1,0:T(8,128)S(1)} %bitcast_add_fusion.2, s32[]{:T(128)} %constant.69.clone.1..sunk, s32[]{:T(128)S(6)} %select_n.125, s32[]{:T(128)S(6)} %select_n.126) | dynamic-update-slice | bytes 1048580 | tf_op jit(solution)/shard_map/while/body/eval_jaxpr/dynamic_update_slice | solution.py:139
  173.2 6.9 %dynamic_update_slice.8 = f32[2,512,384]{2,1,0:T(8,128)S(1)} dynamic-update-slice(f32[2,512,384]{2,1,0:T(8,128)S(1)} %get-tuple-element.259, f32[2,256,256]{2,1,0:T(8,128)S(1)} %bitcast_add_fusion.2, s32[]{:T(128)} %constant.69.clone.1..sunk, s32[]{:T(128)S(6)} %select_n.125, s32[]{:T(128)S(6)} %select_n.126) | dynamic-update-slice | bytes 1048580 | tf_op jit(solution)/shard_map/while/body/eval_jaxpr/dynamic_update_slice | solution.py:139
  186.6 9.2 %dynamic_update_slice.8 = f32[2,512,384]{2,1,0:T(8,128)S(1)} dynamic-update-slice(f32[2,512,384]{2,1,0:T(8,128)S(1)} %get-tuple-element.259, f32[2,256,256]{2,1,0:T(8,128)S(1)} %bitcast_add_fusion.2, s32[]{:T(128)} %constant.69.clone.1..sunk, s32[]{:T(128)S(6)} %select_n.125, s32[]{:T(128)S(6)} %select_n.126) | dynamic-update-slice | bytes 1048580 | tf_op jit(solution)/shard_map/while/body/eval_jaxpr/dynamic_update_slice | solution.py:139
  202.1 8.7 %dynamic_update_slice.8 = f32[2,512,384]{2,1,0:T(8,128)S(1)} dynamic-update-slice(f32[2,512,384]{2,1,0:T(8,128)S(1)} %get-tuple-element.259, f32[2,256,256]{2,1,0:T(8,128)S(1)} %bitcast_add_fusion.2, s32[]{:T(128)} %constant.69.clone.1..sunk, s32[]{:T(128)S(6)} %select_n.125, s32[]{:T(128)S(6)} %select_n.126) | dynamic-update-slice | bytes 1048580 | tf_op jit(solution)/shard_map/while/body/eval_jaxpr/dynamic_update_slice | solution.py:139
  217.1 8.1 %dynamic_update_slice.8 = f32[2,512,384]{2,1,0:T(8,128)S(1)} dynamic-update-slice(f32[2,512,384]{2,1,0:T(8,128)S(1)} %get-tuple-element.259, f32[2,256,256]{2,1,0:T(8,128)S(1)} %bitcast_add_fusion.2, s32[]{:T(128)} %constant.69.clone.1..sunk, s32[]{:T(128)S(6)} %select_n.125, s32[]{:T(128)S(6)} %select_n.126) | dynamic-update-slice | bytes 1048580 | tf_op jit(solution)/shard_map/while/body/eval_jaxpr/dynamic_update_slice | solution.py:139
  231.6 7.3 %dynamic_update_slice.8 = f32[2,512,384]{2,1,0:T(8,128)S(1)} dynamic-update-slice(f32[2,512,384]{2,1,0:T(8,128)S(1)} %get-tuple-element.259, f32[2,256,256]{2,1,0:T(8,128)S(1)} %bitcast_add_fusion.2, s32[]{:T(128)} %constant.69.clone.1..sunk, s32[]{:T(128)S(6)} %select_n.125, s32[]{:T(128)S(6)} %select_n.126) | dynamic-update-slice | bytes 1048580 | tf_op jit(solution)/shard_map/while/body/eval_jaxpr/dynamic_update_slice | solution.py:139
  245.3 8.8 %dynamic_update_slice.8 = f32[2,512,384]{2,1,0:T(8,128)S(1)} dynamic-update-slice(f32[2,512,384]{2,1,0:T(8,128)S(1)} %get-tuple-element.259, f32[2,256,256]{2,1,0:T(8,128)S(1)} %bitcast_add_fusion.2, s32[]{:T(128)} %constant.69.clone.1..sunk, s32[]{:T(128)S(6)} %select_n.125, s32[]{:T(128)S(6)} %select_n.126) | dynamic-update-slice | bytes 1048580 | tf_op jit(solution)/shard_map/while/body/eval_jaxpr/dynamic_update_slice | solution.py:139
  255.6 72.7 %all-reduce.11.cloned.1.call-done = (f32[2,512,384]{2,1,0:T(8,128)}, f32[2,256,256]{2,1,0:T(8,128)}) async-done(((f32[2,512,384]{2,1,0:T(8,128)}, f32[2,256,256]{2,1,0:T(8,128)}), (f32[2,512,384]{2,1,0:T(8,128)}, f32[2,256,256]{2,1,0:T(8,128)})) %all-reduce.11.cloned.1.call-update) | async-done | bytes 2097168 | tf_op jit(solution)/shard_map/psum | solution.py:143
  337.9 4.6 %collective-permute-start.7 = (f32[2,128,128]{2,1,0:T(8,128)S(1)}, f32[2,128,128]{2,1,0:T(8,128)S(1)}, u32[]{:S(2)}, u32[]{:S(2)}) collective-permute-start(f32[2,128,128]{2,1,0:T(8,128)S(1)} %get-tuple-element.151), channel_id=1, source_target_pairs={{0,2},{2,4},{4,6},{1,3},{3,5},{5,7},{8,10},{10,12},{12,14},{9,11},... | collective-permute-start | bytes 393224 | tf_op jit(solution)/shard_map/ppermute | solution.py:12
  342.5 9.4 %psum.62 = f32[]{:T(128)} all-reduce(f32[]{:T(128)} %get-tuple-element.146), channel_id=1, replica_groups=mesh['beam'=4,'row'=4,'col'=2] {'beam'}, use_global_device_ids=true, to_apply=%region_14.15 | all-reduce | flops 1 | bytes 8 | tf_op jit(solution)/shard_map/psum | solution.py:143
  352.6 38.5 %all-reduce.9.cloned.1.call-done = f32[2,256,256]{2,1,0:T(8,128)} async-done(((f32[2,256,256]{2,1,0:T(8,128)}), f32[2,256,256]{2,1,0:T(8,128)}) %all-reduce.9.cloned.1.call-update) | async-done | bytes 524304 | tf_op jit(solution)/shard_map/psum | solution.py:144
  393.0 14.3 %all-reduce.2 = (f32[]{:T(128)}, f32[]{:T(128)}) all-reduce(f32[]{:T(128)} %multiply_reduce_fusion, f32[]{:T(128)} %psum.62), channel_id=1, replica_groups=mesh['beam'=4,'row'=4,'col'=2] {'row','col'}, use_global_device_ids=true, to_apply=%region_8.9 | all-reduce | flops 2 | bytes 16 | tf_op jit(solution)/shard_map/psum | solution.py:146
  (116 shorter events, 79.5 us)
Async XLA Ops:
  7.2 6.3 %copy-start.8 = (s32[1,1,8]{2,1,0:T(1,128)S(1)}, s32[1,1,8]{2,1,0:T(1,128)}, u32[]{:S(2)}) copy-start(s32[1,1,8]{2,1,0:T(1,128)} %param.12) | copy-start | bytes 100
  7.2 6.3 %copy-start.9 = (s32[1,1,8]{2,1,0:T(1,128)S(1)}, s32[1,1,8]{2,1,0:T(1,128)}, u32[]{:S(2)}) copy-start(s32[1,1,8]{2,1,0:T(1,128)} %param.13) | copy-start | bytes 100
  7.2 50.1 %all-reduce.13.cloned.1.call-start = ((), (), s32[]{:S(2)}) async-start(), calls=%async_computation.2 | async-start | bytes 524288 | tf_op jit(solution)/shard_map/psum | solution.py:66
  11.3 317.0 %all-reduce.11.cloned.1.call-start = ((), (), s32[]{:S(2)}) async-start(), calls=%async_computation.1 | async-start | bytes 4194304 | tf_op jit(solution)/shard_map/psum | solution.py:143
  59.2 6.8 %collective-permute-start = (f32[2,128,128]{2,1,0:T(8,128)S(1)}, f32[2,128,128]{2,1,0:T(8,128)S(1)}, u32[]{:S(2)}, u32[]{:S(2)}) collective-permute-start(f32[2,128,128]{2,1,0:T(8,128)S(1)} %get-tuple-element.162), channel_id=1, source_target_pairs={{0,2},{2,4},{4,6},{1,3},{3,5},{5,7},{8,10},{10,12},{12,14},{9,11},... | collective-permute-start | bytes 393224 | tf_op jit(solution)/shard_map/ppermute | solution.py:23
  62.6 6.9 %collective-permute-start.1 = (f32[2,128,128]{2,1,0:T(8,128)S(1)}, f32[2,128,128]{2,1,0:T(8,128)S(1)}, u32[]{:S(2)}, u32[]{:S(2)}) collective-permute-start(f32[2,128,128]{2,1,0:T(8,128)S(1)} %get-tuple-element.163), channel_id=1, source_target_pairs={{2,0},{4,2},{6,4},{3,1},{5,3},{7,5},{10,8},{12,10},{14,12},{11,9},... | collective-permute-start | bytes 393224 | tf_op jit(solution)/shard_map/ppermute | solution.py:25
  64.9 9.4 %copy-start.3 = (f32[2,256,256]{2,1,0:T(8,128)S(1)}, f32[2,256,256]{2,1,0:T(8,128)}, u32[]{:S(2)}) copy-start(f32[2,256,256]{2,1,0:T(8,128)} %param.10) | copy-start | bytes 1572868
  69.5 4.9 %collective-permute-start.2 = (f32[2,512,128]{2,1,0:T(8,128)S(1)}, f32[2,512,128]{2,1,0:T(8,128)S(1)}, u32[]{:S(2)}, u32[]{:S(2)}) collective-permute-start(f32[2,512,128]{2,1,0:T(8,128)S(1)} %pad_maximum_fusion.2), channel_id=1, source_target_pairs={{0,1},{2,3},{4,5},{6,7},{8,9},{10,11},{12,13},{14,15},{16,17},{18,... | collective-permute-start | bytes 1572872 | tf_op jit(solution)/shard_map/ppermute | solution.py:23
  70.8 3.9 collective-permute-start.3
  107.8 1.7 copy-start.1
  107.8 1.7 copy-start.6
  107.8 1.7 copy-start.7
  115.5 4.5 %copy-start.2 = (f32[8,256,512]{2,1,0:T(8,128)S(1)}, f32[8,256,512]{2,1,0:T(8,128)}, u32[]{:S(2)}) copy-start(f32[8,256,512]{2,1,0:T(8,128)} %convolution_bitcast_fusion.1) | copy-start | bytes 12582916
  121.9 4.0 copy-start.4
  121.9 4.0 copy-start.5
  254.2 1.4 copy-start
  255.6 135.5 %all-reduce.9.cloned.1.call-start = ((), (), s32[]{:S(2)}) async-start(), calls=%async_computation | async-start | bytes 1048576 | tf_op jit(solution)/shard_map/psum | solution.py:144
  329.6 4.4 %collective-permute-start.4 = (f32[2,512,128]{2,1,0:T(8,128)S(1)}, f32[2,512,128]{2,1,0:T(8,128)S(1)}, u32[]{:S(2)}, u32[]{:S(2)}) collective-permute-start(f32[2,512,128]{2,1,0:T(8,128)S(1)} %get-tuple-element.148), channel_id=1, source_target_pairs={{1,0},{3,2},{5,4},{7,6},{9,8},{11,10},{13,12},{15,14},{17,16},{19,... | collective-permute-start | bytes 1572872 | tf_op jit(solution)/shard_map/ppermute | solution.py:12
  330.9 4.6 %collective-permute-start.5 = (f32[2,512,128]{2,1,0:T(8,128)S(1)}, f32[2,512,128]{2,1,0:T(8,128)S(1)}, u32[]{:S(2)}, u32[]{:S(2)}) collective-permute-start(f32[2,512,128]{2,1,0:T(8,128)S(1)} %get-tuple-element.149), channel_id=1, source_target_pairs={{0,1},{2,3},{4,5},{6,7},{8,9},{10,11},{12,13},{14,15},{16,17},{18,... | collective-permute-start | bytes 1572872 | tf_op jit(solution)/shard_map/ppermute | solution.py:12
  336.6 15.3 %collective-permute-start.6 = (f32[2,128,128]{2,1,0:T(8,128)S(1)}, f32[2,128,128]{2,1,0:T(8,128)S(1)}, u32[]{:S(2)}, u32[]{:S(2)}) collective-permute-start(f32[2,128,128]{2,1,0:T(8,128)S(1)} %get-tuple-element.150), channel_id=1, source_target_pairs={{2,0},{4,2},{6,4},{3,1},{5,3},{7,5},{10,8},{12,10},{14,12},{11,9},... | collective-permute-start | bytes 393224 | tf_op jit(solution)/shard_map/ppermute | solution.py:12
  337.9 14.0 %collective-permute-start.7 = (f32[2,128,128]{2,1,0:T(8,128)S(1)}, f32[2,128,128]{2,1,0:T(8,128)S(1)}, u32[]{:S(2)}, u32[]{:S(2)}) collective-permute-start(f32[2,128,128]{2,1,0:T(8,128)S(1)} %get-tuple-element.151), channel_id=1, source_target_pairs={{0,2},{2,4},{4,6},{1,3},{3,5},{5,7},{8,10},{10,12},{12,14},{9,11},... | collective-permute-start | bytes 393224 | tf_op jit(solution)/shard_map/ppermute | solution.py:12
Sparse Core Ops, SparseCore 0:
  11.5 45.8 all-reduce.12
  255.7 72.6 all-reduce.10
  334.2 56.8 all-reduce.8
where the time goes:
time: 418 us; the launch traced here: 417 us
  waiting for transfers between devices  160 us (38%)
  local copies, waits for them, and re-layouts  104 us (25%)
  other arithmetic  51.2 us (12%)
  loops' own time  31.3 us (7%)
  blocking collectives  23.7 us (6%)
  starting transfers between devices  17.8 us (4%)
  between operations  16.5 us (4%)
  matrix products  11.9 us (3%)
    psum x1, waiting for transfers between devices, local(): lax.psum((canvas, probe_term, misfit), 'beam')  72.7 us
    dynamic_update_slice x8, local copies, waits for them, and re-layouts, add_window(): return lax.dynamic_update_slice(canvas_now, piece + cells[index], where)  64.8 us
    psum x1, waiting for transfers between devices, local(): phase_sum, absorb_sum = lax.psum((phase_part, absorb_part), 'beam')  43.8 us
    psum x1, waiting for transfers between devices, local(): lax.psum((probe_part, misfit_part), ('row', 'col'))  38.5 us
    another operation x1, loops' own time, local(): canvas = lax.fori_loop(0, count, add_window, canvas)  31.3 us
    gather x24, local copies, waits for them, and re-layouts  21.9 us
    psum x1, blocking collectives, local(): square_sum = lax.psum(jnp.sum(gradient * gradient), ('row', 'col'))  14.3 us
    another operation x2, other arithmetic  11.4 us
  transfers between devices with their start and end apart: 11, of which 6 were waited for; matrix products, arithmetic and copies ran while one was open for 2% of the time, Pallas kernels for 0%

commit v1 on v0

v1 whole, which is shorter than its diff:
```python
import functools
import math

import jax
import jax.numpy as jnp
import numpy as np
from jax import lax
from jax.experimental import pallas as pl
from jax.experimental.pallas import tpu as pltpu
from jax.sharding import PartitionSpec as P


def from_behind(value, axis, steps):
    count = lax.axis_size(axis)
    first, last = (max(0, -steps), min(count, count - steps))
    return lax.ppermute(value, axis, [(source, source + steps) for source in range(first, last)])


def extended(cells, sides, width):
    for axis, dim in sides:
        count = lax.axis_size(axis)
        ends = count - 1
        head = lax.slice_in_dim(cells, 0, width, axis=dim)
        tail = lax.slice_in_dim(cells, cells.shape[dim] - width, cells.shape[dim], axis=dim)
        cells = jnp.concatenate(
            [
                lax.ppermute(tail, axis, [(i, (i + 1) % count) for i in range(ends)]),
                cells,
                lax.ppermute(head, axis, [((i + 1) % count, i) for i in range(ends)]),
            ],
            axis=dim,
        )
    return cells


def dft_matrices(length):
    indices = np.arange(length, dtype=np.int32)
    product = indices[:, None] * indices[None, :] % length
    angles = product.astype(np.float32) * np.float32(2.0 * math.pi / length)
    factor = np.float32(1.0 / math.sqrt(length))
    real = (np.cos(angles) * factor).astype(jnp.bfloat16)
    imag = (-np.sin(angles) * factor).astype(jnp.bfloat16)
    left = np.block([[real, -imag], [imag, real]])
    right = np.block([[real, imag], [-imag, real]])
    return jnp.asarray(left), jnp.asarray(right)


def fold_rims(canvas, half):
    rows_inner = canvas.shape[1] - 2 * half
    cols_inner = canvas.shape[2] - 2 * half
    middle = canvas[:, :, half : half + cols_inner]
    from_right = from_behind(canvas[:, :, :half], "col", -1)
    from_left = from_behind(canvas[:, :, half + cols_inner :], "col", 1)
    middle = middle + from_right
    middle = middle + from_left
    center = middle[:, half : half + rows_inner, :]
    from_below = from_behind(middle[:, :half, :], "row", -1)
    from_above = from_behind(middle[:, half + rows_inner :, :], "row", 1)
    center = center + jnp.pad(from_below, ((0, 0), (rows_inner - half, 0), (0, 0)))
    return center + jnp.pad(from_above, ((0, 0), (0, rows_inner - half), (0, 0)))


def window_kernel(
    rows_ref, cols_ref, trans_ref, probe_ref, amplitude_ref, left_ref, right_ref,
    canvas_ref, term_ref, misfit_ref,
):
    step = pl.program_id(0)
    length = probe_ref.shape[1]
    wide = trans_ref.shape[2]
    row_at = rows_ref[step]
    col_at = cols_ref[step]

    @pl.when(step == 0)
    def _():
        canvas_ref[...] = jnp.zeros_like(canvas_ref)
        term_ref[...] = jnp.zeros_like(term_ref)
        misfit_ref[...] = jnp.zeros_like(misfit_ref)

    row_base = pl.multiple_of(row_at // 8 * 8, 8)
    row_rest = row_at % 8
    back_by = lax.rem(wide - col_at, wide)

    def window(part):
        rows = trans_ref[part, pl.ds(row_base, length + 8), :]
        rows = pltpu.roll(rows, length + 8 - row_rest, 0)[:length]
        return pltpu.roll(rows, back_by, 1)[:, :length]

    dot = functools.partial(jnp.dot, preferred_element_type=jnp.float32)
    trans_real = window(0)
    trans_imag = window(1)
    wave_real = probe_ref[0] * trans_real - probe_ref[1] * trans_imag
    wave_imag = probe_ref[0] * trans_imag + probe_ref[1] * trans_real
    outgoing = jnp.concatenate([wave_real, wave_imag], axis=0).astype(jnp.bfloat16)
    half = dot(left_ref[...], outgoing).astype(jnp.bfloat16)
    far = dot(jnp.concatenate([half[:length], half[length:]], axis=1), right_ref[...])
    far_real = far[:, :length]
    far_imag = far[:, length:]
    amplitude = amplitude_ref[0].astype(jnp.float32)
    modulus = jnp.sqrt(far_real * far_real + far_imag * far_imag)
    off = modulus - amplitude
    misfit_ref[...] += jnp.sum((off * off).reshape(length // 8, 8, length), axis=0)
    ratio = 1.0 - amplitude / jnp.maximum(modulus, 0.5)
    residual = jnp.concatenate([far_real * ratio, far_imag * ratio], axis=0)
    back = dot(right_ref[...], residual.astype(jnp.bfloat16)).astype(jnp.bfloat16)
    near = dot(jnp.concatenate([back[:length], back[length:]], axis=1), left_ref[...])
    grad_real = near[:, :length]
    grad_imag = near[:, length:]
    trans_real = window(0)
    trans_imag = window(1)
    wave_real = probe_ref[0] * trans_real - probe_ref[1] * trans_imag
    wave_imag = probe_ref[0] * trans_imag + probe_ref[1] * trans_real
    term_ref[0] += trans_real * grad_real + trans_imag * grad_imag
    term_ref[1] += trans_real * grad_imag - trans_imag * grad_real
    side = jnp.zeros((length, wide - length), jnp.float32)
    below = jnp.zeros((8, wide), jnp.float32)

    def spread(part, values):
        placed = pltpu.roll(jnp.concatenate([values, side], axis=1), col_at, 1)
        placed = pltpu.roll(jnp.concatenate([placed, below], axis=0), row_rest, 0)
        canvas_ref[part, pl.ds(row_base, length + 8), :] += placed

    spread(0, wave_real * grad_imag - wave_imag * grad_real)
    spread(1, -(wave_real * grad_real + wave_imag * grad_imag))


def window_terms(trans, probe, amplitude, rows, cols):
    count, length = amplitude.shape[:2]
    left, right = dft_matrices(length)
    whole = lambda array: pl.BlockSpec(array.shape, lambda s, r, c: (0,) * array.ndim)
    outs = [
        jax.ShapeDtypeStruct(trans.shape, jnp.float32),
        jax.ShapeDtypeStruct(probe.shape, jnp.float32),
        jax.ShapeDtypeStruct((8, length), jnp.float32),
    ]
    return pl.pallas_call(
        window_kernel,
        out_shape=outs,
        grid_spec=pltpu.PrefetchScalarGridSpec(
            num_scalar_prefetch=2,
            grid=(count,),
            in_specs=[
                whole(trans),
                whole(probe),
                pl.BlockSpec((1, length, length), lambda s, r, c: (s, 0, 0)),
                whole(left),
                whole(right),
            ],
            out_specs=[whole(out) for out in outs],
        ),
        compiler_params=pltpu.CompilerParams(
            dimension_semantics=("arbitrary",), vmem_limit_bytes=48 * 2**20
        ),
    )(rows, cols, trans, probe, amplitude, left, right)


def local(phase_volume, absorb_volume, probe, amplitudes, scan_rows, scan_cols):
    length = probe.shape[1]
    half = length // 2
    count = scan_rows.shape[2]
    rows_local = phase_volume.shape[1]
    cols_local = phase_volume.shape[2]
    phase_part = jnp.sum(phase_volume, axis=0, dtype=jnp.float32)
    absorb_part = jnp.sum(absorb_volume, axis=0, dtype=jnp.float32)
    phase_sum, absorb_sum = lax.psum((phase_part, absorb_part), "beam")
    padded = extended(jnp.stack([phase_sum, absorb_sum]), (("row", 1), ("col", 2)), half)
    damping = jnp.exp(-padded[1])
    trans = jnp.stack([damping * jnp.cos(padded[0]), damping * jnp.sin(padded[0])])
    canvas, probe_term, misfit = window_terms(
        trans, probe, amplitudes.reshape(count, length, length),
        scan_rows.reshape(count), scan_cols.reshape(count),
    )
    summed, probe_part, misfit_part = lax.psum((canvas, probe_term, jnp.sum(misfit)), "beam")
    probe_total, misfit_total = lax.psum((probe_part, misfit_part), ("row", "col"))
    gradient = fold_rims(summed, half)
    square_sum = lax.psum(jnp.sum(gradient * gradient), ("row", "col"))
    plane_devices = lax.axis_size("row") * lax.axis_size("col")
    mean_square = square_sum / (2 * rows_local * cols_local * plane_devices)
    factor = jnp.minimum(1.0, 0.5 / jnp.sqrt(mean_square + 1e-06))
    total = plane_devices * lax.axis_size("beam") * count
    return (gradient * factor, probe_total / total, misfit_total / (total * length * length))


def solution(mesh):
    in_specs = (
        P("beam", "row", "col"),
        P("beam", "row", "col"),
        P(),
        P("row", "col", "beam", None, None),
        P("row", "col", "beam"),
        P("row", "col", "beam"),
    )
    out_specs = (P(None, "row", "col"), P(), P())
    return jax.shard_map(local, mesh=mesh, in_specs=in_specs, out_specs=out_specs, check_vma=False)
```

time: 418 us -> 262 us (0.63)
  local copies, waits for them, and re-layouts: 104 us -> 4.1 us
  other arithmetic: 51.2 us -> 12.2 us
  loops' own time: 31.3 us -> 0 us
  Pallas kernels: 0 us -> 23.2 us
  matrix products: 11.9 us -> 0 us
    dynamic_update_slice x8 -> x0, local copies, waits for them, and re-layouts: 64.8 us -> none  [add_window(): return lax.dynamic_update_slice(canvas_now, piece + cells[index], where)]
    another operation x2 -> x0, loops' own time: 31.3 us -> none  [the longest x1 31.3 us: local(): canvas = lax.fori_loop(0, count, add_window, canvas)]
    pallas_call x0 -> x1, Pallas kernels: none -> 23.2 us  [window_terms(): pl.pallas_call(window_kernel, out_shape=outs, grid_spec=pltpu.PrefetchSca...]
    gather x24 -> x0, local copies, waits for them, and re-layouts: 21.9 us -> none
    another operation x6 -> x1, other arithmetic: 16.4 us -> 1.25 us  [local(): jnp.stack([damping * jnp.cos(padded[0]), damping * jnp.sin(padded[0])])]
    dot_general x2 -> x0, matrix products: 11.9 us -> none  [the longest x1 5.95 us: local(): jnp.einsum('sxab,xbd->sad', half_wave, forward_right, preferred_element_t...]
    add x8 -> x0, other arithmetic: 10.1 us -> none  [add_window(): return lax.dynamic_update_slice(canvas_now, piece + cells[index], where)]
    dynamic_slice x16 -> x0, local copies, waits for them, and re-layouts: 9.42 us -> none  [add_window(): where = (zero_index, row_begin[index], col_begin[index])]
  transfers between devices with their start and end apart: 11 -> 11, of which waited for: 6 -> 7; matrix products, arithmetic and copies ran while one was open for 2% -> 1% of each run, Pallas kernels for 0% -> 0%
where the time goes in v1:
time: 262 us; the launch traced here: 261 us
  waiting for transfers between devices  162 us (62%)
  blocking collectives  23.8 us (9%)
  Pallas kernels  23.2 us (9%)
  starting transfers between devices  19.4 us (7%)
  between operations  16.4 us (6%)
  other arithmetic  12.2 us (5%)
  local copies, waits for them, and re-layouts  4.1 us (2%)
    psum x1, waiting for transfers between devices, local(): lax.psum((canvas, probe_term, jnp.sum(misfit)), 'beam')  68.7 us
    psum x1, waiting for transfers between devices, local(): phase_sum, absorb_sum = lax.psum((phase_part, absorb_part), 'beam')  47.1 us
    psum x1, waiting for transfers between devices, local(): lax.psum((probe_part, misfit_part), ('row', 'col'))  37.7 us
    pallas_call x1, Pallas kernels, window_terms(): pl.pallas_call(window_kernel, out_shape=outs, grid_spec=pltpu.PrefetchSca...  23.2 us
    psum x1, blocking collectives, local(): square_sum = lax.psum(jnp.sum(gradient * gradient), ('row', 'col'))  14.3 us
    ppermute x4, starting transfers between devices, from_behind(): lax.ppermute(value, axis, [(source, source + steps) for source in range(f...  10.2 us
    psum x1, blocking collectives, local(): lax.psum((canvas, probe_term, jnp.sum(misfit)), 'beam')  9.54 us
    ppermute x2, starting transfers between devices, extended(): lax.ppermute(tail, axis, [(i, (i + 1) % count) for i in range(ends)])  6.49 us
  transfers between devices with their start and end apart: 11, of which 7 were waited for; matrix products, arithmetic and copies ran while one was open for 1% of the time, Pallas kernels for 0%

profile of v1, /device:TPU:0, one launch (start us, length us, event | category | flops | bytes accessed | tf_op | source)
XLA Modules:
  0.0 261.3 jit_solution(17365200709027013078)
XLA Ops:
  7.2 2.1 convert_reduce_fusion.1
  10.2 47.1 %all-reduce.13.cloned.1.call-done = (f32[1,256,128]{2,1,0:T(8,128)}, f32[1,256,128]{2,1,0:T(8,128)}) async-done(((f32[1,256,128]{2,1,0:T(8,128)}, f32[1,256,128]{2,1,0:T(8,128)}), (f32[1,256,128]{2,1,0:T(8,128)}, f32[1,256,128]{2,1,0:T(8,128)})) %all-reduce.13.cloned.1.call-update) | async-done | bytes 262160 | tf_op jit(solution)/shard_map/psum | solution.py:164
  59.2 3.4 %collective-permute-start = (f32[2,128,128]{2,1,0:T(8,128)S(1)}, f32[2,128,128]{2,1,0:T(8,128)S(1)}, u32[]{:S(2)}, u32[]{:S(2)}) collective-permute-start(f32[2,128,128]{2,1,0:T(8,128)S(1)} %get-tuple-element.21), channel_id=1, source_target_pairs={{0,2},{2,4},{4,6},{1,3},{3,5},{5,7},{8,10},{10,12},{12,14},{9,11},... | collective-permute-start | bytes 393224 | tf_op jit(solution)/shard_map/ppermute | solution.py:27
  62.6 1.3 collective-permute-start.1
  63.9 1.2 collective-permute-done
  65.1 4.4 %collective-permute-done.1 = f32[2,128,128]{2,1,0:T(8,128)S(1)} collective-permute-done((f32[2,128,128]{2,1,0:T(8,128)S(1)}, f32[2,128,128]{2,1,0:T(8,128)S(1)}, u32[]{:S(2)}, u32[]{:S(2)}) %collective-permute-start.1) | collective-permute-done | bytes 131104 | tf_op jit(solution)/shard_map/ppermute | solution.py:29
  69.5 1.3 collective-permute-start.3
  70.8 3.1 %collective-permute-start.2 = (f32[2,512,128]{2,1,0:T(8,128)S(1)}, f32[2,512,128]{2,1,0:T(8,128)S(1)}, u32[]{:S(2)}, u32[]{:S(2)}) collective-permute-start(f32[2,512,128]{2,1,0:T(8,128)S(1)} %pad_maximum_fusion.2), channel_id=1, source_target_pairs={{0,1},{2,3},{4,5},{6,7},{8,9},{10,11},{12,13},{14,15},{16,17},{18,... | collective-permute-start | bytes 1572872 | tf_op jit(solution)/shard_map/ppermute | solution.py:27
  73.9 1.5 collective-permute-done.2
  75.5 2.9 %cosine_multiply_fusion = (f32[1,512,384]{2,1,0:T(8,128)S(1)}, f32[1,512,384]{2,1,0:T(8,128)S(1)}) fusion(f32[2,512,384]{2,1,0:T(8,128)S(1)} %pad_maximum_fusion), kind=kLoop, calls=%fused_computation.7 | loop fusion | flops 589824 | bytes 3145728 | tf_op jit(solution)/shard_map/mul | solution.py:167
  78.5 1.2 pad_maximum_fusion.1.trans_ref
  80.6 23.2 %shard_map.103 = (f32[2,512,384]{2,1,0:T(8,128)}, f32[2,256,256]{2,1,0:T(8,128)}, f32[8,256]{1,0:T(8,128)S(1)}) custom-call(s32[8]{0:T(128)S(1)} %bitcast.6, s32[8]{0:T(128)S(1)} %bitcast.7, f32[2,512,384]{2,1,0:T(8,128)} %pad_maximum_fusion.1.trans_ref, f32[2,256,256]{2,1,0:T(8,128)S(1)} %copy-done.1, bf16[8,256,256]{2,1,0:T(8,128)(2,1)S(1)} %bitcast.5, ...), custom_call_target="tpu_custom_call" | custom-call | tf_op jit(solution)/shard_map/pallas_call | solution.py:135
  103.9 68.7 %all-reduce.11.cloned.1.call-done = (f32[2,512,384]{2,1,0:T(8,128)}, f32[2,256,256]{2,1,0:T(8,128)}) async-done(((f32[2,512,384]{2,1,0:T(8,128)}, f32[2,256,256]{2,1,0:T(8,128)}), (f32[2,512,384]{2,1,0:T(8,128)}, f32[2,256,256]{2,1,0:T(8,128)})) %all-reduce.11.cloned.1.call-update) | async-done | bytes 2097168 | tf_op jit(solution)/shard_map/psum | solution.py:172
  172.6 1.3 fusion.3
  173.9 1.3 collective-permute-start.4
  175.2 3.1 %collective-permute-start.5 = (f32[2,512,128]{2,1,0:T(8,128)S(1)}, f32[2,512,128]{2,1,0:T(8,128)S(1)}, u32[]{:S(2)}, u32[]{:S(2)}) collective-permute-start(f32[2,512,128]{2,1,0:T(8,128)S(1)} %get-tuple-element.16), channel_id=1, source_target_pairs={{0,1},{2,3},{4,5},{6,7},{8,9},{10,11},{12,13},{14,15},{16,17},{18,... | collective-permute-start | bytes 1572872 | tf_op jit(solution)/shard_map/ppermute | solution.py:16
  178.4 1.5 collective-permute-done.5
  179.8 1.2 fusion.1
  181.0 1.3 collective-permute-start.6
  182.3 4.6 %collective-permute-start.7 = (f32[2,128,128]{2,1,0:T(8,128)S(1)}, f32[2,128,128]{2,1,0:T(8,128)S(1)}, u32[]{:S(2)}, u32[]{:S(2)}) collective-permute-start(f32[2,128,128]{2,1,0:T(8,128)S(1)} %get-tuple-element.20), channel_id=1, source_target_pairs={{0,2},{2,4},{4,6},{1,3},{3,5},{5,7},{8,10},{10,12},{12,14},{9,11},... | collective-permute-start | bytes 393224 | tf_op jit(solution)/shard_map/ppermute | solution.py:16
  187.5 9.5 %psum.62 = f32[]{:T(128)} all-reduce(f32[]{:T(128)} %reduce_sum.39), channel_id=1, replica_groups=mesh['beam'=4,'row'=4,'col'=2] {'beam'}, use_global_device_ids=true, to_apply=%region_10.11 | all-reduce | flops 1 | bytes 8 | tf_op jit(solution)/shard_map/psum | solution.py:172
  197.7 37.7 %all-reduce.9.cloned.1.call-done = f32[2,256,256]{2,1,0:T(8,128)} async-done(((f32[2,256,256]{2,1,0:T(8,128)}), f32[2,256,256]{2,1,0:T(8,128)}) %all-reduce.9.cloned.1.call-update) | async-done | bytes 524304 | tf_op jit(solution)/shard_map/psum | solution.py:173
  235.4 1.9 broadcast_multiply_fusion
  237.3 14.3 %all-reduce.2 = (f32[]{:T(128)}, f32[]{:T(128)}) all-reduce(f32[]{:T(128)} %multiply_reduce_fusion, f32[]{:T(128)} %psum.62), channel_id=1, replica_groups=mesh['beam'=4,'row'=4,'col'=2] {'row','col'}, use_global_device_ids=true, to_apply=%region_6.0 | all-reduce | flops 2 | bytes 16 | tf_op jit(solution)/shard_map/psum | solution.py:175
  (34 shorter events, 5.9 us)
Async XLA Ops:
  7.2 2.2 copy-start.6
  7.2 50.1 %all-reduce.13.cloned.1.call-start = ((), (), s32[]{:S(2)}) async-start(), calls=%async_computation.2 | async-start | bytes 524288 | tf_op jit(solution)/shard_map/psum | solution.py:164
  10.2 162.5 %all-reduce.11.cloned.1.call-start = ((), (), s32[]{:S(2)}) async-start(), calls=%async_computation.1 | async-start | bytes 4194304 | tf_op jit(solution)/shard_map/psum | solution.py:172
  59.2 5.9 %collective-permute-start = (f32[2,128,128]{2,1,0:T(8,128)S(1)}, f32[2,128,128]{2,1,0:T(8,128)S(1)}, u32[]{:S(2)}, u32[]{:S(2)}) collective-permute-start(f32[2,128,128]{2,1,0:T(8,128)S(1)} %get-tuple-element.21), channel_id=1, source_target_pairs={{0,2},{2,4},{4,6},{1,3},{3,5},{5,7},{8,10},{10,12},{12,14},{9,11},... | collective-permute-start | bytes 393224 | tf_op jit(solution)/shard_map/ppermute | solution.py:27
  62.6 6.9 %collective-permute-start.1 = (f32[2,128,128]{2,1,0:T(8,128)S(1)}, f32[2,128,128]{2,1,0:T(8,128)S(1)}, u32[]{:S(2)}, u32[]{:S(2)}) collective-permute-start(f32[2,128,128]{2,1,0:T(8,128)S(1)} %get-tuple-element.22), channel_id=1, source_target_pairs={{2,0},{4,2},{6,4},{3,1},{5,3},{7,5},{10,8},{12,10},{14,12},{11,9},... | collective-permute-start | bytes 393224 | tf_op jit(solution)/shard_map/ppermute | solution.py:29
  69.5 4.4 %collective-permute-start.3 = (f32[2,512,128]{2,1,0:T(8,128)S(1)}, f32[2,512,128]{2,1,0:T(8,128)S(1)}, u32[]{:S(2)}, u32[]{:S(2)}) collective-permute-start(f32[2,512,128]{2,1,0:T(8,128)S(1)} %pad_maximum_fusion.2), channel_id=1, source_target_pairs={{1,0},{3,2},{5,4},{7,6},{9,8},{11,10},{13,12},{15,14},{17,16},{19,... | collective-permute-start | bytes 1572872 | tf_op jit(solution)/shard_map/ppermute | solution.py:29
  70.8 4.6 %collective-permute-start.2 = (f32[2,512,128]{2,1,0:T(8,128)S(1)}, f32[2,512,128]{2,1,0:T(8,128)S(1)}, u32[]{:S(2)}, u32[]{:S(2)}) collective-permute-start(f32[2,512,128]{2,1,0:T(8,128)S(1)} %pad_maximum_fusion.2), channel_id=1, source_target_pairs={{0,1},{2,3},{4,5},{6,7},{8,9},{10,11},{12,13},{14,15},{16,17},{18,... | collective-permute-start | bytes 1572872 | tf_op jit(solution)/shard_map/ppermute | solution.py:27
  78.4 1.5 copy-start
  78.4 1.9 copy-start.1
  78.4 2.1 copy-start.2
  78.4 2.2 copy-start.3
  78.4 2.2 copy-start.4
  78.4 2.2 copy-start.5
  103.9 131.5 %all-reduce.9.cloned.1.call-start = ((), (), s32[]{:S(2)}) async-start(), calls=%async_computation | async-start | bytes 1048576 | tf_op jit(solution)/shard_map/psum | solution.py:173
  173.9 4.4 %collective-permute-start.4 = (f32[2,512,128]{2,1,0:T(8,128)S(1)}, f32[2,512,128]{2,1,0:T(8,128)S(1)}, u32[]{:S(2)}, u32[]{:S(2)}) collective-permute-start(f32[2,512,128]{2,1,0:T(8,128)S(1)} %get-tuple-element.15), channel_id=1, source_target_pairs={{1,0},{3,2},{5,4},{7,6},{9,8},{11,10},{13,12},{15,14},{17,16},{19,... | collective-permute-start | bytes 1572872 | tf_op jit(solution)/shard_map/ppermute | solution.py:16
  175.2 4.6 %collective-permute-start.5 = (f32[2,512,128]{2,1,0:T(8,128)S(1)}, f32[2,512,128]{2,1,0:T(8,128)S(1)}, u32[]{:S(2)}, u32[]{:S(2)}) collective-permute-start(f32[2,512,128]{2,1,0:T(8,128)S(1)} %get-tuple-element.16), channel_id=1, source_target_pairs={{0,1},{2,3},{4,5},{6,7},{8,9},{10,11},{12,13},{14,15},{16,17},{18,... | collective-permute-start | bytes 1572872 | tf_op jit(solution)/shard_map/ppermute | solution.py:16
  181.0 16.0 %collective-permute-start.6 = (f32[2,128,128]{2,1,0:T(8,128)S(1)}, f32[2,128,128]{2,1,0:T(8,128)S(1)}, u32[]{:S(2)}, u32[]{:S(2)}) collective-permute-start(f32[2,128,128]{2,1,0:T(8,128)S(1)} %get-tuple-element.19), channel_id=1, source_target_pairs={{2,0},{4,2},{6,4},{3,1},{5,3},{7,5},{10,8},{12,10},{14,12},{11,9},... | collective-permute-start | bytes 393224 | tf_op jit(solution)/shard_map/ppermute | solution.py:16
  182.3 14.7 %collective-permute-start.7 = (f32[2,128,128]{2,1,0:T(8,128)S(1)}, f32[2,128,128]{2,1,0:T(8,128)S(1)}, u32[]{:S(2)}, u32[]{:S(2)}) collective-permute-start(f32[2,128,128]{2,1,0:T(8,128)S(1)} %get-tuple-element.20), channel_id=1, source_target_pairs={{0,2},{2,4},{4,6},{1,3},{3,5},{5,7},{8,10},{10,12},{12,14},{9,11},... | collective-permute-start | bytes 393224 | tf_op jit(solution)/shard_map/ppermute | solution.py:16
Sparse Core Ops, SparseCore 0:
  11.5 45.8 all-reduce.12
  104.0 68.5 all-reduce.10
  178.5 56.8 all-reduce.8

commit v2 on v1

--- a/solution.py
+++ b/solution.py
@@ -8,29 +8,6 @@
 from jax.experimental import pallas as pl
 from jax.experimental.pallas import tpu as pltpu
 from jax.sharding import PartitionSpec as P
-
-
-def from_behind(value, axis, steps):
-    count = lax.axis_size(axis)
-    first, last = (max(0, -steps), min(count, count - steps))
-    return lax.ppermute(value, axis, [(source, source + steps) for source in range(first, last)])
-
-
-def extended(cells, sides, width):
-    for axis, dim in sides:
-        count = lax.axis_size(axis)
-        ends = count - 1
-        head = lax.slice_in_dim(cells, 0, width, axis=dim)
-        tail = lax.slice_in_dim(cells, cells.shape[dim] - width, cells.shape[dim], axis=dim)
-        cells = jnp.concatenate(
-            [
-                lax.ppermute(tail, axis, [(i, (i + 1) % count) for i in range(ends)]),
-                cells,
-                lax.ppermute(head, axis, [((i + 1) % count, i) for i in range(ends)]),
-            ],
-            axis=dim,
-        )
-    return cells
 
 
 def dft_matrices(length):
@@ -43,21 +20,6 @@
     left = np.block([[real, -imag], [imag, real]])
     right = np.block([[real, imag], [-imag, real]])
     return jnp.asarray(left), jnp.asarray(right)
-
-
-def fold_rims(canvas, half):
-    rows_inner = canvas.shape[1] - 2 * half
-    cols_inner = canvas.shape[2] - 2 * half
-    middle = canvas[:, :, half : half + cols_inner]
-    from_right = from_behind(canvas[:, :, :half], "col", -1)
-    from_left = from_behind(canvas[:, :, half + cols_inner :], "col", 1)
-    middle = middle + from_right
-    middle = middle + from_left
-    center = middle[:, half : half + rows_inner, :]
-    from_below = from_behind(middle[:, :half, :], "row", -1)
-    from_above = from_behind(middle[:, half + rows_inner :, :], "row", 1)
-    center = center + jnp.pad(from_below, ((0, 0), (rows_inner - half, 0), (0, 0)))
-    return center + jnp.pad(from_above, ((0, 0), (0, rows_inner - half), (0, 0)))
 
 
 def window_kernel(
@@ -153,31 +115,323 @@
     )(rows, cols, trans, probe, amplitude, left, right)
 
 
+class Sends:
+    def __init__(self, axes, send_sem, recv_sem):
+        self.axes, self.sends, self.recvs, self.used = axes, send_sem, recv_sem, 0
+
+    def greet(self):
+        barrier = pltpu.get_barrier_semaphore()
+        peers = 0
+        for axis, (me, count) in self.axes.items():
+            for d in range(1, count):
+                pl.semaphore_signal(
+                    barrier, inc=1, device_id={axis: lax.rem(me + d, count)},
+                    device_id_type=pl.DeviceIdType.MESH,
+                )
+                peers += 1
+        pl.semaphore_wait(barrier, peers)
+
+    def copy(self, axis, peer, src, dst):
+        index = self.used
+        self.used += 1
+        return pltpu.make_async_remote_copy(
+            src_ref=src, dst_ref=dst, send_sem=self.sends.at[index],
+            recv_sem=self.recvs.at[index], device_id={axis: peer},
+            device_id_type=pl.DeviceIdType.MESH,
+        )
+
+    def each(self, axis, source, target):
+        me, count = self.axes[axis]
+        copies = []
+        for d in range(1, count):
+            peer = lax.rem(me + d, count)
+            one = self.copy(axis, peer, source(peer), target(d - 1))
+            one.start()
+            copies.append(one)
+        return copies
+
+    def sides(self, axis, down, up):
+        me, count = self.axes[axis]
+        before = self.copy(axis, lax.rem(me + count - 1, count), *down)
+        after = self.copy(axis, lax.rem(me + 1, count), *up)
+        pl.when(me > 0)(before.start)
+        pl.when(me < count - 1)(after.start)
+
+        def finish():
+            pl.when(me > 0)(before.wait_send)
+            pl.when(me < count - 1)(after.wait_send)
+            pl.when(me < count - 1)(before.wait_recv)
+            pl.when(me > 0)(after.wait_recv)
+
+        return finish
+
+
+def wait_all(copies):
+    for one in copies:
+        one.wait()
+
+
+def axes_of(sizes):
+    return {axis: (lax.axis_index(axis), count) for axis, count in sizes}
+
+
+def project_kernel(sizes, half, phase_ref, absorb_ref, out_ref, part, slots, piece, tile, strip, side, send_sem, recv_sem):
+    axes = axes_of(sizes)
+    net = Sends(axes, send_sem, recv_sem)
+    beam, beams = axes["beam"]
+    row, rows_count = axes["row"]
+    col, cols_count = axes["col"]
+    depth, rows, cols = phase_ref.shape
+    share = rows // beams
+    strip[0] = jnp.ones(strip.shape[1:], jnp.float32)
+    strip[1] = jnp.zeros(strip.shape[1:], jnp.float32)
+    side[:, 0] = jnp.ones((2,) + strip.shape[1:], jnp.float32)
+    side[:, 1] = jnp.zeros((2,) + strip.shape[1:], jnp.float32)
+    net.greet()
+    for plane, ref in enumerate((phase_ref, absorb_ref)):
+        total = ref[0].astype(jnp.float32)
+        for d in range(1, depth):
+            total += ref[d].astype(jnp.float32)
+        part[:, plane] = total.reshape(beams, share, cols)
+    scatter = net.each("beam", lambda peer: part.at[peer], lambda d: slots.at[d])
+    wait_all(scatter)
+    total = part[beam]
+    for d in range(beams - 1):
+        total += slots[d]
+    damping = jnp.exp(-total[1])
+    piece[0] = damping * jnp.cos(total[0])
+    piece[1] = damping * jnp.sin(total[0])
+    tile[beam] = piece[...]
+    gather = net.each("beam", lambda peer: piece, lambda d: tile.at[beam])
+    wait_all(gather)
+    for q in range(beams):
+        strip[:, half + q * share : half + (q + 1) * share] = tile[q]
+    finish = net.sides(
+        "row",
+        (strip.at[:, pl.ds(half, half)], strip.at[:, pl.ds(half + rows, half)]),
+        (strip.at[:, pl.ds(rows, half)], strip.at[:, pl.ds(0, half)]),
+    )
+    finish()
+    finish = net.sides("col", (strip, side.at[1]), (strip, side.at[0]))
+    out_ref[:, :, half : half + cols] = strip[...]
+    finish()
+    out_ref[:, :, :half] = side[0][:, :, cols - half :]
+    out_ref[:, :, half + cols :] = side[1][:, :, :half]
+
+
+def comm_params(number):
+    return pltpu.CompilerParams(
+        collective_id=number, has_side_effects=True, vmem_limit_bytes=48 * 2**20
+    )
+
+
+def vmem_specs(count):
+    return [pl.BlockSpec(memory_space=pltpu.VMEM)] * count
+
+
+def project(sizes, half, phase_volume, absorb_volume):
+    depth, rows, cols = phase_volume.shape
+    beams = dict(sizes)["beam"]
+    share = rows // beams
+    f32 = jnp.float32
+    wires = sum(count for _, count in sizes) * 2
+    tall = rows + 2 * half
+    return pl.pallas_call(
+        functools.partial(project_kernel, sizes, half),
+        out_shape=jax.ShapeDtypeStruct((2, tall, cols + 2 * half), f32),
+        in_specs=vmem_specs(2),
+        out_specs=vmem_specs(1)[0],
+        scratch_shapes=[
+            pltpu.VMEM((beams, 2, share, cols), f32),
+            pltpu.VMEM((beams - 1, 2, share, cols), f32),
+            pltpu.VMEM((2, share, cols), f32),
+            pltpu.VMEM((beams, 2, share, cols), f32),
+            pltpu.VMEM((2, tall, cols), f32),
+            pltpu.VMEM((2, 2, tall, cols), f32),
+            pltpu.SemaphoreType.DMA((wires,)),
+            pltpu.SemaphoreType.DMA((wires,)),
+        ],
+        compiler_params=comm_params(1),
+    )(phase_volume, absorb_volume)
+
+
+def combine_kernel(
+    sizes, half, entries, positions, canvas_ref, term_ref, misfit_ref,
+    step_ref, probe_ref, loss_ref,
+    left, right, side, strip, strip_in, folded, rims, mine, grads,
+    term_col, term_a, term_beam, term_b, term_row, result, small, small_sum,
+    send_sem, recv_sem,
+):
+    axes = axes_of(sizes)
+    net = Sends(axes, send_sem, recv_sem)
+    beam, beams = axes["beam"]
+    row, rows_count = axes["row"]
+    col, cols_count = axes["col"]
+    blocks = strip.shape[1]
+    cols = strip.shape[4]
+    rims[...] = jnp.zeros_like(rims)
+    net.greet()
+    left[...] = canvas_ref[:, :, :half]
+    right[...] = canvas_ref[:, :, half + cols :]
+    finish = net.sides("col", (left, side.at[1]), (right, side.at[0]))
+    term_copies = net.each("col", lambda peer: term_ref.at[peer], lambda d: term_col.at[d])
+    side_zero = jnp.zeros(side.shape[1:], jnp.float32)
+
+    @pl.when(col == 0)
+    def _():
+        side[0] = side_zero
+
+    @pl.when(col == cols_count - 1)
+    def _():
+        side[1] = side_zero
+
+    finish()
+    folded_now = canvas_ref[:, :, half : half + cols]
+    lower = folded_now[:, :, :half] + side[0]
+    strip[...] = (lower + side[1]).reshape(strip.shape)
+    grid_copies = net.each("beam", lambda peer: strip.at[:, :, peer], lambda d: strip_in.at[d])
+    wait_all(term_copies)
+    total = term_ref[col]
+    for d in range(cols_count - 1):
+        total += term_col[d]
+    term_a[...] = total
+    term_copies = net.each("beam", lambda peer: term_a.at[peer], lambda d: term_beam.at[d])
+    wait_all(grid_copies)
+    total = strip[:, :, beam]
+    for d in range(beams - 1):
+        total += strip_in[d]
+    folded[...] = total
+    finish = net.sides(
+        "row",
+        (folded.at[:, 0], rims.at[1]),
+        (folded.at[:, blocks - 1], rims.at[0]),
+    )
+    wait_all(term_copies)
+    total = term_a[beam]
+    for d in range(beams - 1):
+        total += term_beam[d]
+    term_b[...] = total
+    term_copies = net.each("row", lambda peer: term_b.at[peer], lambda d: term_row.at[d])
+    finish()
+    mine[...] = folded[:, 1 : blocks - 1]
+    mine[:, 0] += rims[0]
+    mine[:, blocks - 3] += rims[1]
+    grad_copies = net.each("beam", lambda peer: mine, lambda d: grads.at[:, :, beam])
+    values = mine[...]
+    square = jnp.sum((values * values).reshape(-1, 8, cols), axis=0)
+    misfit = misfit_ref[...].reshape(8, misfit_ref.shape[1] // cols, cols)
+    misfit_sum = misfit_ref[:, :cols]
+    for k in range(1, misfit_ref.shape[1] // cols):
+        misfit_sum += misfit_ref[:, k * cols : (k + 1) * cols]
+    small_sum[0, 0] = square
+    small_sum[0, 1] = misfit_sum
+    base = 0
+
+    def share_small(axis, level, base):
+        count = axes[axis][1]
+        return net.each(axis, lambda peer: small_sum.at[level], lambda d: small.at[base + d]), base + count - 1
+
+    def add_small(level, begin, end):
+        total = small_sum[level]
+        for k in range(begin, end):
+            total += small[k]
+        small_sum[level + 1] = total
+
+    small_copies, first = share_small("row", 0, 0)
+    wait_all(term_copies)
+    total = term_b[row]
+    for d in range(rows_count - 1):
+        total += term_row[d]
+    total = total * (1.0 / positions)
+    result[col, beam, row] = total
+    term_copies = net.each("row", lambda peer: result.at[col, beam, row], lambda d: result.at[col, beam, row])
+    wait_all(small_copies)
+    add_small(0, 0, first)
+    small_copies, second = share_small("beam", 1, first)
+    wait_all(term_copies)
+    term_copies = net.each("beam", lambda peer: result.at[col, beam], lambda d: result.at[col, beam])
+    wait_all(small_copies)
+    add_small(1, first, second)
+    small_copies, third = share_small("col", 2, second)
+    wait_all(grad_copies)
+    grads[:, :, beam] = mine[...]
+    wait_all(small_copies)
+    add_small(2, second, third)
+    mean_square = jnp.sum(small_sum[3, 0], keepdims=True) / entries
+    factor = jnp.minimum(1.0, 0.5 / jnp.sqrt(mean_square + 1e-06))
+    step_ref[...] = grads[...] * factor[None, None, None]
+    loss_ref[...] = jnp.broadcast_to(jnp.sum(small_sum[3, 1], keepdims=True), loss_ref.shape)
+    wait_all(term_copies)
+    term_copies = net.each("col", lambda peer: result.at[col], lambda d: result.at[col])
+    wait_all(term_copies)
+    probe_ref[...] = result[...]
+
+
+def combine(sizes, half, rows, cols, positions, canvas, term, misfit):
+    counts = dict(sizes)
+    beams, rows_count, cols_count = counts["beam"], counts["row"], counts["col"]
+    f32 = jnp.float32
+    blocks = rows // half + 2
+    thin = half // beams
+    lines = term.shape[0] * term.shape[1] // (cols_count * beams * rows_count)
+    width = term.shape[2]
+    pieces = (cols_count, beams, rows_count, lines, width)
+    entries = 2 * rows * cols * rows_count * cols_count
+    wires = 4 * sum(counts.values())
+    tall = canvas.shape[1]
+    grid = (2, blocks - 2, beams, thin, cols)
+    step, probe_gradient, loss = pl.pallas_call(
+        functools.partial(combine_kernel, sizes, half, entries, positions),
+        out_shape=[
+            jax.ShapeDtypeStruct(grid, f32),
+            jax.ShapeDtypeStruct(pieces, f32),
+            jax.ShapeDtypeStruct((8, 128), f32),
+        ],
+        in_specs=vmem_specs(3),
+        out_specs=vmem_specs(3),
+        scratch_shapes=[
+            pltpu.VMEM((2, tall, half), f32),
+            pltpu.VMEM((2, tall, half), f32),
+            pltpu.VMEM((2, 2, tall, half), f32),
+            pltpu.VMEM((2, blocks, beams, thin, cols), f32),
+            pltpu.VMEM((beams - 1, 2, blocks, thin, cols), f32),
+            pltpu.VMEM((2, blocks, thin, cols), f32),
+            pltpu.VMEM((2, 2, thin, cols), f32),
+            pltpu.VMEM((2, blocks - 2, thin, cols), f32),
+            pltpu.VMEM(grid, f32),
+            pltpu.VMEM((cols_count - 1,) + pieces[1:], f32),
+            pltpu.VMEM(pieces[1:], f32),
+            pltpu.VMEM((beams - 1,) + pieces[2:], f32),
+            pltpu.VMEM(pieces[2:], f32),
+            pltpu.VMEM((rows_count - 1,) + pieces[3:], f32),
+            pltpu.VMEM(pieces, f32),
+            pltpu.VMEM((sum(counts.values()), 2, 8, cols), f32),
+            pltpu.VMEM((4, 2, 8, cols), f32),
+            pltpu.SemaphoreType.DMA((wires,)),
+            pltpu.SemaphoreType.DMA((wires,)),
+        ],
+        compiler_params=comm_params(2),
+    )(canvas, term.reshape(pieces), misfit)
+    return (
+        step.reshape(2, rows, cols),
+        probe_gradient.reshape(term.shape),
+        loss[0, 0] / (positions * width * width),
+    )
+
+
 def local(phase_volume, absorb_volume, probe, amplitudes, scan_rows, scan_cols):
     length = probe.shape[1]
     half = length // 2
     count = scan_rows.shape[2]
-    rows_local = phase_volume.shape[1]
-    cols_local = phase_volume.shape[2]
-    phase_part = jnp.sum(phase_volume, axis=0, dtype=jnp.float32)
-    absorb_part = jnp.sum(absorb_volume, axis=0, dtype=jnp.float32)
-    phase_sum, absorb_sum = lax.psum((phase_part, absorb_part), "beam")
-    padded = extended(jnp.stack([phase_sum, absorb_sum]), (("row", 1), ("col", 2)), half)
-    damping = jnp.exp(-padded[1])
-    trans = jnp.stack([damping * jnp.cos(padded[0]), damping * jnp.sin(padded[0])])
-    canvas, probe_term, misfit = window_terms(
+    rows, cols = phase_volume.shape[1:]
+    sizes = tuple((axis, lax.axis_size(axis)) for axis in ("beam", "row", "col"))
+    trans = project(sizes, half, phase_volume, absorb_volume)
+    canvas, term, misfit = window_terms(
         trans, probe, amplitudes.reshape(count, length, length),
         scan_rows.reshape(count), scan_cols.reshape(count),
     )
-    summed, probe_part, misfit_part = lax.psum((canvas, probe_term, jnp.sum(misfit)), "beam")
-    probe_total, misfit_total = lax.psum((probe_part, misfit_part), ("row", "col"))
-    gradient = fold_rims(summed, half)
-    square_sum = lax.psum(jnp.sum(gradient * gradient), ("row", "col"))
-    plane_devices = lax.axis_size("row") * lax.axis_size("col")
-    mean_square = square_sum / (2 * rows_local * cols_local * plane_devices)
-    factor = jnp.minimum(1.0, 0.5 / jnp.sqrt(mean_square + 1e-06))
-    total = plane_devices * lax.axis_size("beam") * count
-    return (gradient * factor, probe_total / total, misfit_total / (total * length * length))
+    positions = count * math.prod(size for _, size in sizes)
+    return combine(sizes, half, rows, cols, positions, canvas, term, misfit)
 
 
 def solution(mesh):

time: 262 us -> 79.3 us (0.30)
  waiting for transfers between devices: 162 us -> 0 us
  Pallas kernels: 23.2 us -> 70.9 us
  blocking collectives: 23.8 us -> 0 us
  starting transfers between devices: 19.4 us -> 0 us
  between operations: 16.4 us -> 2.5 us
  other arithmetic: 12.2 us -> 0 us
    psum x3 -> x0, waiting for transfers between devices: 154 us -> none  [the longest x1 68.7 us: local(): lax.psum((canvas, probe_term, jnp.sum(misfit)), 'beam')]
    pallas_call x0 -> x2, Pallas kernels: none -> 48.9 us  [the longest x1 28.6 us: combine(): pl.pallas_call(functools.partial(combine_kernel, sizes, half, entries, po...]
    psum x2 -> x0, blocking collectives: 23.8 us -> none  [the longest x1 14.3 us: local(): square_sum = lax.psum(jnp.sum(gradient * gradient), ('row', 'col'))]
    ppermute x8 -> x0, starting transfers between devices: 19.3 us -> none  [the longest x4 10.2 us: from_behind(): lax.ppermute(value, axis, [(source, source + steps) for source in range(f...]
    ppermute x8 -> x0, waiting for transfers between devices: 8.5 us -> none  [the longest x2 4.37 us: extended(): lax.ppermute(head, axis, [((i + 1) % count, i) for i in range(ends)])]
    reduce_sum x4 -> x0, other arithmetic: 4.17 us -> none  [the longest x1 2.11 us: local(): phase_part = jnp.sum(phase_volume, axis=0, dtype=jnp.float32)]
    mul x2 -> x0, other arithmetic: 3.64 us -> none  [the longest x1 2.9 us: local(): damping * jnp.cos(padded[0])]
    unnamed x15 -> x20, local copies, waits for them, and re-layouts: 1.87 us -> 5.11 us
  transfers between devices with their start and end apart: 11 -> 0, of which waited for: 7 -> 0; matrix products, arithmetic and copies ran while one was open for 1% -> 0% of each run, Pallas kernels for 0% -> 0%
where the time goes in v2:
time: 79.3 us; the launch traced here: 79.1 us
  Pallas kernels  70.9 us (89%)
  local copies, waits for them, and re-layouts  5.62 us (7%)
  between operations  2.5 us (3%)
    pallas_call x1, Pallas kernels, combine(): pl.pallas_call(functools.partial(combine_kernel, sizes, half, entries, po...  28.6 us
    pallas_call x1, Pallas kernels, window_terms(): pl.pallas_call(window_kernel, out_shape=outs, grid_spec=pltpu.PrefetchSca...  22.1 us
    pallas_call x1, Pallas kernels, project(): pl.pallas_call(functools.partial(project_kernel, sizes, half), out_shape=...  20.3 us
    unnamed x20, local copies, waits for them, and re-layouts  5.11 us

profile of v2, /device:TPU:0, one launch (start us, length us, event | category | flops | bytes accessed | tf_op | source)
XLA Modules:
  0.0 79.1 jit_solution(5765378368841966905)
XLA Ops:
  0.6 0.0 copy-start.1
  0.6 1.2 %copy-done.1 = bf16[16,256,128]{2,1,0:T(8,128)(2,1)S(1)} copy-done((bf16[16,256,128]{2,1,0:T(8,128)(2,1)S(1)}, bf16[16,256,128]{2,1,0:T(8,128)(2,1)}, u32[]{:S(2)}) %copy-start.1) | copy-done | bytes 1048600
  1.9 0.0 copy-start.2
  1.9 1.2 %copy-done.2 = bf16[16,256,128]{2,1,0:T(8,128)(2,1)S(1)} copy-done((bf16[16,256,128]{2,1,0:T(8,128)(2,1)S(1)}, bf16[16,256,128]{2,1,0:T(8,128)(2,1)}, u32[]{:S(2)}) %copy-start.2) | copy-done | bytes 1048600
  3.1 0.0 copy-start.3
  3.1 0.0 copy-start.4
  3.1 0.0 copy-start.5
  3.1 0.0 copy-start.6
  3.1 0.0 copy-start.7
  3.1 0.0 copy-start.8
  3.1 20.3 %shard_map.103.trans_ref = f32[2,512,384]{2,1,0:T(8,128)S(1)} custom-call(bf16[16,256,128]{2,1,0:T(8,128)(2,1)S(1)} %copy-done.1, bf16[16,256,128]{2,1,0:T(8,128)(2,1)S(1)} %copy-done.2), custom_call_target="tpu_custom_call" | custom-call | tf_op jit(solution)/shard_map/pallas_call | solution.py:239
  23.4 0.0 copy-start
  23.4 1.1 %copy-done = f32[2,512,384]{2,1,0:T(8,128)} copy-done((f32[2,512,384]{2,1,0:T(8,128)}, f32[2,512,384]{2,1,0:T(8,128)S(1)}, u32[]{:S(2)}) %copy-start) | copy-done | bytes 1572888
  24.6 0.0 copy-done.3
  24.6 0.0 copy-done.4
  24.6 0.0 copy-done.5
  24.6 0.0 copy-done.6
  24.6 0.0 copy-done.7
  24.6 0.0 copy-done.8
  24.6 22.1 %shard_map.104 = (f32[2,512,384]{2,1,0:T(8,128)S(1)}, f32[2,256,256]{2,1,0:T(8,128)S(1)}, f32[8,256]{1,0:T(8,128)S(1)}) custom-call(s32[8]{0:T(128)S(1)} %bitcast.11, s32[8]{0:T(128)S(1)} %bitcast.12, f32[2,512,384]{2,1,0:T(8,128)} %copy-done, f32[2,256,256]{2,1,0:T(8,128)S(1)} %copy-done.4, bf16[8,256,256]{2,1,0:T(8,128)(2,1)S(1)} %bitcast.7, ...), custom_call_target="tpu_custom_call" | custom-call | tf_op jit(solution)/shard_map/pallas_call | solution.py:97
  46.7 28.6 %shard_map.105 = (f32[2,2,4,32,128]{4,3,2,1,0:T(8,128)S(1)}, f32[2,4,4,16,256]{4,3,2,1,0:T(8,128)S(1)}, f32[8,128]{1,0:T(8,128)S(1)}) custom-call(f32[2,512,384]{2,1,0:T(8,128)S(1)} %get-tuple-element.9.canvas_ref, f32[2,4,4,16,256]{4,3,2,1,0:T(8,128)S(1)} %bitcast.9, f32[8,256]{1,0:T(8,128)S(1)} %get-tuple-element.11.misfit_ref), custom_call_target="tpu_custom_call" | custom-call | tf_op jit(solution)/shard_map/pallas_call | solution.py:383
  75.3 0.5 slice.3
  76.4 0.7 copy.13
  77.1 0.8 %copy.14 = f32[2,256,256]{2,1,0:T(8,128)} copy(f32[2,256,256]{2,1,0:T(8,128)S(1)} %bitcast.8) | data formatting | bytes 1048576
Async XLA Ops:
  0.6 1.2 %copy-start.1 = (bf16[16,256,128]{2,1,0:T(8,128)(2,1)S(1)}, bf16[16,256,128]{2,1,0:T(8,128)(2,1)}, u32[]{:S(2)}) copy-start(bf16[16,256,128]{2,1,0:T(8,128)(2,1)} %phase_ref.1) | copy-start | bytes 3145732
  1.9 1.2 %copy-start.2 = (bf16[16,256,128]{2,1,0:T(8,128)(2,1)S(1)}, bf16[16,256,128]{2,1,0:T(8,128)(2,1)}, u32[]{:S(2)}) copy-start(bf16[16,256,128]{2,1,0:T(8,128)(2,1)} %absorb_ref.1) | copy-start | bytes 3145732
  3.1 21.5 %copy-start.3 = (bf16[1,1,8,256,256]{4,3,2,1,0:T(8,128)(2,1)S(1)}, bf16[1,1,8,256,256]{4,3,2,1,0:T(8,128)(2,1)}, u32[]{:S(2)}) copy-start(bf16[1,1,8,256,256]{4,3,2,1,0:T(8,128)(2,1)} %param.11) | copy-start | bytes 3145732
  3.1 21.5 %copy-start.4 = (f32[2,256,256]{2,1,0:T(8,128)S(1)}, f32[2,256,256]{2,1,0:T(8,128)}, u32[]{:S(2)}) copy-start(f32[2,256,256]{2,1,0:T(8,128)} %probe_ref.1) | copy-start | bytes 1572868
  3.1 21.5 %copy-start.5 = (bf16[512,512]{1,0:T(8,128)(2,1)S(1)}, bf16[512,512]{1,0:T(8,128)(2,1)}, u32[]{:S(2)}) copy-start(bf16[512,512]{1,0:T(8,128)(2,1)} %constant.9.clone.right_ref) | copy-start | bytes 1572868
  3.1 21.5 %copy-start.6 = (bf16[512,512]{1,0:T(8,128)(2,1)S(1)}, bf16[512,512]{1,0:T(8,128)(2,1)}, u32[]{:S(2)}) copy-start(bf16[512,512]{1,0:T(8,128)(2,1)} %constant.8.clone.left_ref) | copy-start | bytes 1572868
  3.1 21.5 %copy-start.7 = (s32[1,1,8]{2,1,0:T(1,128)S(1)}, s32[1,1,8]{2,1,0:T(1,128)}, u32[]{:S(2)}) copy-start(s32[1,1,8]{2,1,0:T(1,128)} %param.12) | copy-start | bytes 100
  3.1 21.5 %copy-start.8 = (s32[1,1,8]{2,1,0:T(1,128)S(1)}, s32[1,1,8]{2,1,0:T(1,128)}, u32[]{:S(2)}) copy-start(s32[1,1,8]{2,1,0:T(1,128)} %param.13) | copy-start | bytes 100
  23.4 1.2 %copy-start = (f32[2,512,384]{2,1,0:T(8,128)}, f32[2,512,384]{2,1,0:T(8,128)S(1)}, u32[]{:S(2)}) copy-start(f32[2,512,384]{2,1,0:T(8,128)S(1)} %shard_map.103.trans_ref) | copy-start | bytes 4718596

commit v3 on v2

--- a/solution.py
+++ b/solution.py
@@ -24,13 +24,13 @@
 
 def window_kernel(
     rows_ref, cols_ref, trans_ref, probe_ref, amplitude_ref, left_ref, right_ref,
-    canvas_ref, term_ref, misfit_ref,
+    canvas_ref, term_ref, misfit_ref, kept,
 ):
     step = pl.program_id(0)
+    pair = amplitude_ref.shape[0]
     length = probe_ref.shape[1]
     wide = trans_ref.shape[2]
-    row_at = rows_ref[step]
-    col_at = cols_ref[step]
+    dot = functools.partial(jnp.dot, preferred_element_type=jnp.float32)
 
     @pl.when(step == 0)
     def _():
@@ -38,55 +38,70 @@
         term_ref[...] = jnp.zeros_like(term_ref)
         misfit_ref[...] = jnp.zeros_like(misfit_ref)
 
-    row_base = pl.multiple_of(row_at // 8 * 8, 8)
-    row_rest = row_at % 8
-    back_by = lax.rem(wide - col_at, wide)
-
-    def window(part):
-        rows = trans_ref[part, pl.ds(row_base, length + 8), :]
-        rows = pltpu.roll(rows, length + 8 - row_rest, 0)[:length]
-        return pltpu.roll(rows, back_by, 1)[:, :length]
-
-    dot = functools.partial(jnp.dot, preferred_element_type=jnp.float32)
-    trans_real = window(0)
-    trans_imag = window(1)
-    wave_real = probe_ref[0] * trans_real - probe_ref[1] * trans_imag
-    wave_imag = probe_ref[0] * trans_imag + probe_ref[1] * trans_real
-    outgoing = jnp.concatenate([wave_real, wave_imag], axis=0).astype(jnp.bfloat16)
-    half = dot(left_ref[...], outgoing).astype(jnp.bfloat16)
-    far = dot(jnp.concatenate([half[:length], half[length:]], axis=1), right_ref[...])
-    far_real = far[:, :length]
-    far_imag = far[:, length:]
-    amplitude = amplitude_ref[0].astype(jnp.float32)
-    modulus = jnp.sqrt(far_real * far_real + far_imag * far_imag)
-    off = modulus - amplitude
-    misfit_ref[...] += jnp.sum((off * off).reshape(length // 8, 8, length), axis=0)
-    ratio = 1.0 - amplitude / jnp.maximum(modulus, 0.5)
-    residual = jnp.concatenate([far_real * ratio, far_imag * ratio], axis=0)
-    back = dot(right_ref[...], residual.astype(jnp.bfloat16)).astype(jnp.bfloat16)
-    near = dot(jnp.concatenate([back[:length], back[length:]], axis=1), left_ref[...])
-    grad_real = near[:, :length]
-    grad_imag = near[:, length:]
-    trans_real = window(0)
-    trans_imag = window(1)
-    wave_real = probe_ref[0] * trans_real - probe_ref[1] * trans_imag
-    wave_imag = probe_ref[0] * trans_imag + probe_ref[1] * trans_real
-    term_ref[0] += trans_real * grad_real + trans_imag * grad_imag
-    term_ref[1] += trans_real * grad_imag - trans_imag * grad_real
-    side = jnp.zeros((length, wide - length), jnp.float32)
-    below = jnp.zeros((8, wide), jnp.float32)
-
-    def spread(part, values):
-        placed = pltpu.roll(jnp.concatenate([values, side], axis=1), col_at, 1)
-        placed = pltpu.roll(jnp.concatenate([placed, below], axis=0), row_rest, 0)
-        canvas_ref[part, pl.ds(row_base, length + 8), :] += placed
-
-    spread(0, wave_real * grad_imag - wave_imag * grad_real)
-    spread(1, -(wave_real * grad_real + wave_imag * grad_imag))
+    def place(which):
+        row_at = rows_ref[step * pair + which]
+        col_at = cols_ref[step * pair + which]
+        return pl.multiple_of(row_at // 8 * 8, 8), row_at % 8, col_at
+
+    def wave(which):
+        trans_real, trans_imag = kept[which, 0], kept[which, 1]
+        wave_real = probe_ref[0] * trans_real - probe_ref[1] * trans_imag
+        wave_imag = probe_ref[0] * trans_imag + probe_ref[1] * trans_real
+        return trans_real, trans_imag, wave_real, wave_imag
+
+    def enter(which):
+        row_base, row_rest, col_at = place(which)
+        for part in range(2):
+            rows = trans_ref[part, pl.ds(row_base, length + 8), :]
+            rows = pltpu.roll(rows, length + 8 - row_rest, 0)[:length]
+            kept[which, part] = pltpu.roll(rows, lax.rem(wide - col_at, wide), 1)[:, :length]
+        _, _, wave_real, wave_imag = wave(which)
+        return jnp.concatenate([wave_real, wave_imag], axis=0).astype(jnp.bfloat16)
+
+    def transform(first, second, values):
+        part = dot(first[...], values).astype(jnp.bfloat16)
+        return dot(jnp.concatenate([part[:length], part[length:]], axis=1), second[...])
+
+    def compare(which, far):
+        far_real = far[:, :length]
+        far_imag = far[:, length:]
+        amplitude = amplitude_ref[which].astype(jnp.float32)
+        modulus = jnp.sqrt(far_real * far_real + far_imag * far_imag)
+        off = modulus - amplitude
+        misfit_ref[...] += jnp.sum((off * off).reshape(length // 8, 8, length), axis=0)
+        ratio = 1.0 - amplitude / jnp.maximum(modulus, 0.5)
+        residual = jnp.concatenate([far_real * ratio, far_imag * ratio], axis=0)
+        return residual.astype(jnp.bfloat16)
+
+    def leave(which, near):
+        row_base, row_rest, col_at = place(which)
+        grad_real = near[:, :length]
+        grad_imag = near[:, length:]
+        trans_real, trans_imag, wave_real, wave_imag = wave(which)
+        term_ref[0] += trans_real * grad_real + trans_imag * grad_imag
+        term_ref[1] += trans_real * grad_imag - trans_imag * grad_real
+        side = jnp.zeros((length, wide - length), jnp.float32)
+        below = jnp.zeros((8, wide), jnp.float32)
+        object_terms = (
+            wave_real * grad_imag - wave_imag * grad_real,
+            -(wave_real * grad_real + wave_imag * grad_imag),
+        )
+        for part, values in enumerate(object_terms):
+            placed = pltpu.roll(jnp.concatenate([values, side], axis=1), col_at, 1)
+            placed = pltpu.roll(jnp.concatenate([placed, below], axis=0), row_rest, 0)
+            canvas_ref[part, pl.ds(row_base, length + 8), :] += placed
+
+    waves = [enter(which) for which in range(pair)]
+    fars = [transform(left_ref, right_ref, wave_now) for wave_now in waves]
+    residuals = [compare(which, fars[which]) for which in range(pair)]
+    nears = [transform(right_ref, left_ref, residual) for residual in residuals]
+    for which in range(pair):
+        leave(which, nears[which])
 
 
 def window_terms(trans, probe, amplitude, rows, cols):
     count, length = amplitude.shape[:2]
+    pair = 2 if count % 2 == 0 else 1
     left, right = dft_matrices(length)
     whole = lambda array: pl.BlockSpec(array.shape, lambda s, r, c: (0,) * array.ndim)
     outs = [
@@ -99,15 +114,16 @@
         out_shape=outs,
         grid_spec=pltpu.PrefetchScalarGridSpec(
             num_scalar_prefetch=2,
-            grid=(count,),
+            grid=(count // pair,),
             in_specs=[
                 whole(trans),
                 whole(probe),
-                pl.BlockSpec((1, length, length), lambda s, r, c: (s, 0, 0)),
+                pl.BlockSpec((pair, length, length), lambda s, r, c: (s, 0, 0)),
                 whole(left),
                 whole(right),
             ],
             out_specs=[whole(out) for out in outs],
+            scratch_shapes=[pltpu.VMEM((pair, 2, length, length), jnp.float32)],
         ),
         compiler_params=pltpu.CompilerParams(
             dimension_semantics=("arbitrary",), vmem_limit_bytes=48 * 2**20
@@ -150,18 +166,20 @@
             copies.append(one)
         return copies
 
-    def sides(self, axis, down, up):
+    def sides(self, axis, down, up, to_before=True, to_after=True):
         me, count = self.axes[axis]
         before = self.copy(axis, lax.rem(me + count - 1, count), *down)
         after = self.copy(axis, lax.rem(me + 1, count), *up)
-        pl.when(me > 0)(before.start)
-        pl.when(me < count - 1)(after.start)
+        has_before, has_after = me > 0, me < count - 1
+        both = jnp.logical_and
+        pl.when(both(has_before, to_before))(before.start)
+        pl.when(both(has_after, to_after))(after.start)
 
         def finish():
-            pl.when(me > 0)(before.wait_send)
-            pl.when(me < count - 1)(after.wait_send)
-            pl.when(me < count - 1)(before.wait_recv)
-            pl.when(me > 0)(after.wait_recv)
+            pl.when(both(has_before, to_before))(before.wait_send)
+            pl.when(both(has_after, to_after))(after.wait_send)
+            pl.when(both(has_after, to_before))(before.wait_recv)
+            pl.when(both(has_before, to_after))(after.wait_recv)
 
         return finish
 
@@ -175,7 +193,7 @@
     return {axis: (lax.axis_index(axis), count) for axis, count in sizes}
 
 
-def project_kernel(sizes, half, phase_ref, absorb_ref, out_ref, part, slots, piece, tile, strip, side, send_sem, recv_sem):
+def project_kernel(sizes, half, phase_ref, absorb_ref, out_ref, part, slots, strip, side, send_sem, recv_sem):
     axes = axes_of(sizes)
     net = Sends(axes, send_sem, recv_sem)
     beam, beams = axes["beam"]
@@ -183,6 +201,7 @@
     col, cols_count = axes["col"]
     depth, rows, cols = phase_ref.shape
     share = rows // beams
+    edge = half // share
     strip[0] = jnp.ones(strip.shape[1:], jnp.float32)
     strip[1] = jnp.zeros(strip.shape[1:], jnp.float32)
     side[:, 0] = jnp.ones((2,) + strip.shape[1:], jnp.float32)
@@ -199,24 +218,31 @@
     for d in range(beams - 1):
         total += slots[d]
     damping = jnp.exp(-total[1])
-    piece[0] = damping * jnp.cos(total[0])
-    piece[1] = damping * jnp.sin(total[0])
-    tile[beam] = piece[...]
-    gather = net.each("beam", lambda peer: piece, lambda d: tile.at[beam])
-    wait_all(gather)
-    for q in range(beams):
-        strip[:, half + q * share : half + (q + 1) * share] = tile[q]
-    finish = net.sides(
-        "row",
-        (strip.at[:, pl.ds(half, half)], strip.at[:, pl.ds(half + rows, half)]),
-        (strip.at[:, pl.ds(rows, half)], strip.at[:, pl.ds(0, half)]),
-    )
+    own = edge + beam
+    strip[0, own] = damping * jnp.cos(total[0])
+    strip[1, own] = damping * jnp.sin(total[0])
+    gather = net.each("beam", lambda peer: strip.at[:, own], lambda d: strip.at[:, own])
+    finishes = []
+    for d in range(beams):
+        if d:
+            gather[d - 1].wait_recv()
+        share_at = lax.rem(beam + beams - d, beams)
+        here = strip.at[:, edge + share_at]
+        finishes.append(net.sides(
+            "row",
+            (here, strip.at[:, lax.rem(edge + beams + share_at, strip.shape[1])]),
+            (here, strip.at[:, lax.rem(edge + share_at + strip.shape[1] - beams, strip.shape[1])]),
+            share_at < edge, share_at >= beams - edge,
+        ))
+    for one in gather:
+        one.wait_send()
+    for finish in finishes:
+        finish()
+    finish = net.sides("col", (strip, side.at[1]), (strip, side.at[0]))
+    out_ref[:, :, half : half + cols] = strip[...].reshape(2, rows + 2 * half, cols)
     finish()
-    finish = net.sides("col", (strip, side.at[1]), (strip, side.at[0]))
-    out_ref[:, :, half : half + cols] = strip[...]
-    finish()
-    out_ref[:, :, :half] = side[0][:, :, cols - half :]
-    out_ref[:, :, half + cols :] = side[1][:, :, :half]
+    out_ref[:, :, :half] = side[0].reshape(2, rows + 2 * half, cols)[:, :, cols - half :]
+    out_ref[:, :, half + cols :] = side[1].reshape(2, rows + 2 * half, cols)[:, :, :half]
 
 
 def comm_params(number):
@@ -234,7 +260,7 @@
     beams = dict(sizes)["beam"]
     share = rows // beams
     f32 = jnp.float32
-    wires = sum(count for _, count in sizes) * 2
+    wires = sum(count for _, count in sizes) * 2 + 2 * beams
     tall = rows + 2 * half
     return pl.pallas_call(
         functools.partial(project_kernel, sizes, half),
@@ -244,10 +270,8 @@
         scratch_shapes=[
             pltpu.VMEM((beams, 2, share, cols), f32),
             pltpu.VMEM((beams - 1, 2, share, cols), f32),
-            pltpu.VMEM((2, share, cols), f32),
-            pltpu.VMEM((beams, 2, share, cols), f32),
-            pltpu.VMEM((2, tall, cols), f32),
-            pltpu.VMEM((2, 2, tall, cols), f32),
+            pltpu.VMEM((2, tall // share, share, cols), f32),
+            pltpu.VMEM((2, 2, tall // share, share, cols), f32),
             pltpu.SemaphoreType.DMA((wires,)),
             pltpu.SemaphoreType.DMA((wires,)),
         ],
@@ -289,37 +313,36 @@
     folded_now = canvas_ref[:, :, half : half + cols]
     lower = folded_now[:, :, :half] + side[0]
     strip[...] = (lower + side[1]).reshape(strip.shape)
-    grid_copies = net.each("beam", lambda peer: strip.at[:, :, peer], lambda d: strip_in.at[d])
+    finish = net.sides(
+        "row",
+        (strip.at[:, 0], rims.at[1]),
+        (strip.at[:, blocks - 1], rims.at[0]),
+    )
     wait_all(term_copies)
     total = term_ref[col]
     for d in range(cols_count - 1):
         total += term_col[d]
     term_a[...] = total
     term_copies = net.each("beam", lambda peer: term_a.at[peer], lambda d: term_beam.at[d])
-    wait_all(grid_copies)
-    total = strip[:, :, beam]
-    for d in range(beams - 1):
-        total += strip_in[d]
-    folded[...] = total
-    finish = net.sides(
-        "row",
-        (folded.at[:, 0], rims.at[1]),
-        (folded.at[:, blocks - 1], rims.at[0]),
-    )
+    finish()
+    folded[...] = strip[:, 1 : blocks - 1]
+    folded[:, 0] += rims[0]
+    folded[:, blocks - 3] += rims[1]
+    grid_copies = net.each("beam", lambda peer: folded.at[:, :, peer], lambda d: strip_in.at[d])
     wait_all(term_copies)
     total = term_a[beam]
     for d in range(beams - 1):
         total += term_beam[d]
     term_b[...] = total
     term_copies = net.each("row", lambda peer: term_b.at[peer], lambda d: term_row.at[d])
-    finish()
-    mine[...] = folded[:, 1 : blocks - 1]
-    mine[:, 0] += rims[0]
-    mine[:, blocks - 3] += rims[1]
+    wait_all(grid_copies)
+    total = folded[:, :, beam]
+    for d in range(beams - 1):
+        total += strip_in[d]
+    mine[...] = total
     grad_copies = net.each("beam", lambda peer: mine, lambda d: grads.at[:, :, beam])
     values = mine[...]
     square = jnp.sum((values * values).reshape(-1, 8, cols), axis=0)
-    misfit = misfit_ref[...].reshape(8, misfit_ref.shape[1] // cols, cols)
     misfit_sum = misfit_ref[:, :cols]
     for k in range(1, misfit_ref.shape[1] // cols):
         misfit_sum += misfit_ref[:, k * cols : (k + 1) * cols]
@@ -394,9 +417,9 @@
             pltpu.VMEM((2, tall, half), f32),
             pltpu.VMEM((2, 2, tall, half), f32),
             pltpu.VMEM((2, blocks, beams, thin, cols), f32),
-            pltpu.VMEM((beams - 1, 2, blocks, thin, cols), f32),
-            pltpu.VMEM((2, blocks, thin, cols), f32),
-            pltpu.VMEM((2, 2, thin, cols), f32),
+            pltpu.VMEM((beams - 1, 2, blocks - 2, thin, cols), f32),
+            pltpu.VMEM(grid, f32),
+            pltpu.VMEM((2, 2, beams, thin, cols), f32),
             pltpu.VMEM((2, blocks - 2, thin, cols), f32),
             pltpu.VMEM(grid, f32),
             pltpu.VMEM((cols_count - 1,) + pieces[1:], f32),

time: 79.3 us -> 67.8 us (0.85)
  Pallas kernels: 70.9 us -> 59.5 us
    pallas_call x1, Pallas kernels: 22.1 us -> 15.9 us  [window_terms(): pl.pallas_call(window_kernel, out_shape=outs, grid_spec=pltpu.PrefetchSca...]
    pallas_call x1, Pallas kernels: 28.6 us -> 23.9 us  [combine(): pl.pallas_call(functools.partial(combine_kernel, sizes, half, entries, po...]
where the time goes in v3:
time: 67.8 us; the launch traced here: 67.6 us
  Pallas kernels  59.5 us (88%)
  local copies, waits for them, and re-layouts  5.62 us (8%)
  between operations  2.5 us (4%)
    pallas_call x1, Pallas kernels, combine(): pl.pallas_call(functools.partial(combine_kernel, sizes, half, entries, po...  23.9 us
    pallas_call x1, Pallas kernels, project(): pl.pallas_call(functools.partial(project_kernel, sizes, half), out_shape=...  19.7 us
    pallas_call x1, Pallas kernels, window_terms(): pl.pallas_call(window_kernel, out_shape=outs, grid_spec=pltpu.PrefetchSca...  15.9 us
    unnamed x20, local copies, waits for them, and re-layouts  5.11 us

profile of v3, /device:TPU:0, one launch (start us, length us, event | category | flops | bytes accessed | tf_op | source)
XLA Modules:
  0.0 67.6 jit_solution(7395018948970303858)
XLA Ops:
  0.6 0.0 copy-start.1
  0.6 1.2 %copy-done.1 = bf16[16,256,128]{2,1,0:T(8,128)(2,1)S(1)} copy-done((bf16[16,256,128]{2,1,0:T(8,128)(2,1)S(1)}, bf16[16,256,128]{2,1,0:T(8,128)(2,1)}, u32[]{:S(2)}) %copy-start.1) | copy-done | bytes 1048600
  1.9 0.0 copy-start.2
  1.9 1.2 %copy-done.2 = bf16[16,256,128]{2,1,0:T(8,128)(2,1)S(1)} copy-done((bf16[16,256,128]{2,1,0:T(8,128)(2,1)S(1)}, bf16[16,256,128]{2,1,0:T(8,128)(2,1)}, u32[]{:S(2)}) %copy-start.2) | copy-done | bytes 1048600
  3.1 0.0 copy-start.3
  3.1 0.0 copy-start.4
  3.1 0.0 copy-start.5
  3.1 0.0 copy-start.6
  3.1 0.0 copy-start.7
  3.1 0.0 copy-start.8
  3.1 19.7 %shard_map.103.trans_ref = f32[2,512,384]{2,1,0:T(8,128)S(1)} custom-call(bf16[16,256,128]{2,1,0:T(8,128)(2,1)S(1)} %copy-done.1, bf16[16,256,128]{2,1,0:T(8,128)(2,1)S(1)} %copy-done.2), custom_call_target="tpu_custom_call" | custom-call | tf_op jit(solution)/shard_map/pallas_call | solution.py:265
  22.9 0.0 copy-start
  22.9 1.1 %copy-done = f32[2,512,384]{2,1,0:T(8,128)} copy-done((f32[2,512,384]{2,1,0:T(8,128)}, f32[2,512,384]{2,1,0:T(8,128)S(1)}, u32[]{:S(2)}) %copy-start) | copy-done | bytes 1572888
  24.0 0.0 copy-done.3
  24.0 0.0 copy-done.4
  24.0 0.0 copy-done.5
  24.0 0.0 copy-done.6
  24.0 0.0 copy-done.7
  24.0 0.0 copy-done.8
  24.0 15.9 %shard_map.104 = (f32[2,512,384]{2,1,0:T(8,128)S(1)}, f32[2,256,256]{2,1,0:T(8,128)S(1)}, f32[8,256]{1,0:T(8,128)S(1)}) custom-call(s32[8]{0:T(128)S(1)} %bitcast.11, s32[8]{0:T(128)S(1)} %bitcast.12, f32[2,512,384]{2,1,0:T(8,128)} %copy-done, f32[2,256,256]{2,1,0:T(8,128)S(1)} %copy-done.4, bf16[8,256,256]{2,1,0:T(8,128)(2,1)S(1)} %bitcast.7, ...), custom_call_target="tpu_custom_call" | custom-call | tf_op jit(solution)/shard_map/pallas_call | solution.py:112
  39.9 23.9 %shard_map.105 = (f32[2,2,4,32,128]{4,3,2,1,0:T(8,128)S(1)}, f32[2,4,4,16,256]{4,3,2,1,0:T(8,128)S(1)}, f32[8,128]{1,0:T(8,128)S(1)}) custom-call(f32[2,512,384]{2,1,0:T(8,128)S(1)} %get-tuple-element.9.canvas_ref, f32[2,4,4,16,256]{4,3,2,1,0:T(8,128)S(1)} %bitcast.9, f32[8,256]{1,0:T(8,128)S(1)} %get-tuple-element.11.misfit_ref), custom_call_target="tpu_custom_call" | custom-call | tf_op jit(solution)/shard_map/pallas_call | solution.py:406
  63.8 0.5 slice.3
  65.0 0.7 %copy.13 = f32[2,256,128]{2,1,0:T(8,128)} copy(f32[2,256,128]{2,1,0:T(8,128)S(1)} %bitcast.10) | data formatting | bytes 524288
  65.7 0.8 %copy.14 = f32[2,256,256]{2,1,0:T(8,128)} copy(f32[2,256,256]{2,1,0:T(8,128)S(1)} %bitcast.8) | data formatting | bytes 1048576
Async XLA Ops:
  0.6 1.2 %copy-start.1 = (bf16[16,256,128]{2,1,0:T(8,128)(2,1)S(1)}, bf16[16,256,128]{2,1,0:T(8,128)(2,1)}, u32[]{:S(2)}) copy-start(bf16[16,256,128]{2,1,0:T(8,128)(2,1)} %phase_ref.1) | copy-start | bytes 3145732
  1.9 1.2 %copy-start.2 = (bf16[16,256,128]{2,1,0:T(8,128)(2,1)S(1)}, bf16[16,256,128]{2,1,0:T(8,128)(2,1)}, u32[]{:S(2)}) copy-start(bf16[16,256,128]{2,1,0:T(8,128)(2,1)} %absorb_ref.1) | copy-start | bytes 3145732
  3.1 20.9 %copy-start.3 = (bf16[1,1,8,256,256]{4,3,2,1,0:T(8,128)(2,1)S(1)}, bf16[1,1,8,256,256]{4,3,2,1,0:T(8,128)(2,1)}, u32[]{:S(2)}) copy-start(bf16[1,1,8,256,256]{4,3,2,1,0:T(8,128)(2,1)} %param.11) | copy-start | bytes 3145732
  3.1 20.9 %copy-start.4 = (f32[2,256,256]{2,1,0:T(8,128)S(1)}, f32[2,256,256]{2,1,0:T(8,128)}, u32[]{:S(2)}) copy-start(f32[2,256,256]{2,1,0:T(8,128)} %probe_ref.1) | copy-start | bytes 1572868
  3.1 20.9 %copy-start.5 = (bf16[512,512]{1,0:T(8,128)(2,1)S(1)}, bf16[512,512]{1,0:T(8,128)(2,1)}, u32[]{:S(2)}) copy-start(bf16[512,512]{1,0:T(8,128)(2,1)} %constant.9.clone.right_ref) | copy-start | bytes 1572868
  3.1 20.9 %copy-start.6 = (bf16[512,512]{1,0:T(8,128)(2,1)S(1)}, bf16[512,512]{1,0:T(8,128)(2,1)}, u32[]{:S(2)}) copy-start(bf16[512,512]{1,0:T(8,128)(2,1)} %constant.8.clone.left_ref) | copy-start | bytes 1572868
  3.1 20.9 %copy-start.7 = (s32[1,1,8]{2,1,0:T(1,128)S(1)}, s32[1,1,8]{2,1,0:T(1,128)}, u32[]{:S(2)}) copy-start(s32[1,1,8]{2,1,0:T(1,128)} %param.12) | copy-start | bytes 100
  3.1 20.9 %copy-start.8 = (s32[1,1,8]{2,1,0:T(1,128)S(1)}, s32[1,1,8]{2,1,0:T(1,128)}, u32[]{:S(2)}) copy-start(s32[1,1,8]{2,1,0:T(1,128)} %param.13) | copy-start | bytes 100
  22.9 1.2 %copy-start = (f32[2,512,384]{2,1,0:T(8,128)}, f32[2,512,384]{2,1,0:T(8,128)S(1)}, u32[]{:S(2)}) copy-start(f32[2,512,384]{2,1,0:T(8,128)S(1)} %shard_map.103.trans_ref) | copy-start | bytes 4718596
